TPU v7x, 32 devices: a whole 2x2x4 slice. The times are simulated.
32 devices in a mesh: ka: 8 (over y, x, core), ga: 4 (over z).
Axes of the slice: x: 2, y: 2, z: 4, core: 2. Of those that a mesh axis runs over, the one named last changes fastest.
Arguments:
- pair_densities: float32 [8192, 8192], P('ka', 'ga'), may hold values from -0.0625 to 0.0625
- energies: float32 [8192], P('ka'), may hold values from -2 to 2
- coulomb: float32 [8192], P('ga'), may hold values from 0.2 to 2
- start: float32 [8192, 128], P('ka'), may hold values from -6 to 6
Outputs:
- alphas: float32 [4, 128], replicated
- betas: float32 [4, 128], replicated
- lanczos_vector: float32 [8192, 128], P('ka')
All inputs are finite; a program needn't handle non-finite values.
Results may differ from a plain program's by a relative error of at most 0.00013.
Values sent between devices are 32-bit elements; how exact they have to be, the bound alone decides.
No kernel may reach another device: no remote copies, remote signals or barrier semaphores. Data moves between devices by JAX's collectives and lax.ppermute only.
A program may use at most 64 MiB of HBM per device.

v0:
```python
import functools

import jax
import jax.numpy as jnp
from jax import lax
from jax.experimental import pallas as pl
from jax.experimental.pallas import tpu as pltpu
from jax.sharding import PartitionSpec as P


ITERS = 4
EPSILON = 1e-06
LANES = 128
KA_CUT = 6
GA_CUTS = (8,)
ROWS = 8
MIB = 1024 * 1024


VMEM = pl.BlockSpec(memory_space=pltpu.VMEM)
SMEM = pl.BlockSpec(memory_space=pltpu.SMEM)
F32, B16 = jnp.float32, jnp.bfloat16

CORE, LEAD, DEPTH, CHIP = range(4)


def call(body, outs, flops, own, *args):
    return pl.pallas_call(
        body,
        out_shape=[jax.ShapeDtypeStruct(shape, dtype) for shape, dtype in outs],
        in_specs=[SMEM] + [VMEM] * len(args),
        out_specs=[VMEM] * len(outs),
        cost_estimate=pl.CostEstimate(flops=flops, bytes_accessed=0, transcendentals=0),
        compiler_params=pltpu.CompilerParams(vmem_limit_bytes=8 * MIB),
    )(own, *args)


def split_matrix(own_ref, m_ref, parts_ref, t_parts_ref, held_ref, arrived):
    rows, cols = m_ref.shape
    tile = min(rows // 2, 128)
    wide = min(cols // 2, 1024)
    copies = []
    for i in range(rows // tile):
        at = pl.ds(i * tile, tile)
        copies.append(pltpu.make_async_copy(m_ref.at[at, :], held_ref.at[at, :], arrived.at[i]))
        copies[-1].start()
    for i in range(rows // tile):
        at = pl.ds(i * tile, tile)
        side, place = divmod(i * tile, rows // 2)
        copies[i].wait()
        for half in range(2):

            def step(j, _):
                to = pl.multiple_of(j * wide, wide)
                x = held_ref[at, pl.ds(pl.multiple_of(half * (cols // 2) + to, wide), wide)]
                hi = x.astype(B16)
                parts_ref[half, at, pl.ds(to, wide)] = hi
                parts_ref[half, at, pl.ds(pl.multiple_of(cols // 2 + to, wide), wide)] = (x - hi.astype(F32)).astype(B16)
                x = x.T
                hi = x.astype(B16)
                down = pl.ds(pl.multiple_of(half * (cols // 2) + to, wide), wide)
                t_parts_ref[side, down, place : place + tile] = hi
                place_lo = rows // 2 + place
                t_parts_ref[side, down, place_lo : place_lo + tile] = (x - hi.astype(F32)).astype(B16)
                return 0

            lax.fori_loop(0, cols // 2 // wide, step, 0)


def half_of(ref, side):
    part = ref.shape[0] // 2
    return ref[pl.ds(pl.multiple_of(side * part, ROWS), part), :]


def two_parts(x):
    hi = x.astype(B16)
    lo = x - hi.astype(F32)
    return jnp.concatenate([hi, lo.astype(B16)], axis=1)


def columns_product(parts_ref, side, rhs):
    both = jnp.dot(parts_ref[side], jnp.concatenate([rhs, rhs], axis=0), preferred_element_type=F32)
    return both[:, :LANES] + both[:, LANES:]


def add_product(parts_ref, side, rhs, base_ref, begin, out_ref, size):
    rows = pl.ds(pl.multiple_of(begin, ROWS), size)
    rhs = jnp.concatenate([rhs, rhs], axis=0)
    both = jnp.dot(parts_ref[side, rows, :], rhs, preferred_element_type=F32)
    out_ref[:size, :] = base_ref[rows, :] + (both[:, :LANES] + both[:, LANES:])


def block_of(rows):
    return jnp.concatenate(rows + [jnp.zeros((ROWS - len(rows), LANES), F32)], axis=0)


def column_sum(x):
    return jnp.sum(x, axis=0, keepdims=True)


def next_rows(energy, mixed, alpha, beta, r, v):
    unit = r * (1.0 / beta)
    return energy * unit + mixed - alpha * unit - beta * v, unit


def advance_own(own_ref, energy_ref, fixed_ref, y_ref, r_ref, v_ref):
    part = r_ref.shape[0]
    alpha = fixed_ref[1:2, :] + column_sum(y_ref[part:, :])
    r, unit = next_rows(
        half_of(energy_ref, own_ref[LEAD]), y_ref[:part, :], alpha, fixed_ref[0:1, :], r_ref[...], v_ref[...]
    )
    return r, unit, alpha


def advance_other(own_ref, energy_ref, fixed_ref, alpha_ref, y_ref, r_ref, v_ref):
    return next_rows(
        half_of(energy_ref, 1 - own_ref[LEAD]), y_ref[...], alpha_ref[...], fixed_ref[0:1, :], r_ref[...], v_ref[...]
    )


def add_both(t_parts_ref, lead, rhs_ref, begin, out_ref, size):
    rows = pl.ds(begin, size)
    total = None
    for n, side in enumerate((lead, 1 - lead)):
        rhs = jnp.concatenate([rhs_ref[n]] * 2, axis=0)
        both = jnp.dot(t_parts_ref[side, rows, :], rhs, preferred_element_type=F32)
        total = both if total is None else total + both
    out_ref[:size, :] = total[:, :LANES] + total[:, LANES:]


def first_send(own_ref, t_parts_ref, energy_ref, start_ref, send_ref, rhs_ref, tail_ref, own_half_ref, other_half_ref, *, chips):
    lead = own_ref[LEAD]
    squares = energies = 0.0
    for n, (side, ref) in enumerate(((lead, own_half_ref), (1 - lead, other_half_ref))):
        r = half_of(start_ref, side)
        ref[...] = r
        rhs_ref[n] = two_parts(r)
        squares = squares + column_sum(r * r)
        energies = energies + column_sum(r * r * half_of(energy_ref, side))
    tail = tail_of(own_ref, tail_ref.shape, squares, energies, chips)
    tail_ref[...] = tail
    part = t_parts_ref.shape[1] // 2
    begin = pl.multiple_of((1 - own_ref[CORE]) * part, ROWS)
    add_both(t_parts_ref, lead, rhs_ref, begin, send_ref, part)
    send_ref[part:, :] = tail


def first_keep(own_ref, t_parts_ref, rhs_ref, tail_ref, keep_ref):
    part = t_parts_ref.shape[1] // 2
    begin = pl.multiple_of(own_ref[CORE] * part, ROWS)
    add_both(t_parts_ref, own_ref[LEAD], rhs_ref, begin, keep_ref, part)
    keep_ref[part:, :] = tail_ref[...]


def tail_of(own_ref, shape, squares, energies, chips):
    row = lax.broadcasted_iota(jnp.int32, shape, 0)
    chip = own_ref[CHIP]
    return jnp.where(row == chip, squares, jnp.where(row == chips + chip, energies, 0.0))


def project_own(own_ref, t_parts_ref, energy_ref, fixed_ref, y_ref, r_ref, v_ref, base_ref, sums_ref, next_ref, unit_ref, alpha_ref):
    r, unit_ref[...], alpha_ref[...] = advance_own(own_ref, energy_ref, fixed_ref, y_ref, r_ref, v_ref)
    next_ref[...] = r
    project_rows(own_ref[LEAD], t_parts_ref, energy_ref, r, base_ref, sums_ref)


def project_rows(side, t_parts_ref, energy_ref, r, base_ref, sums_ref):
    square = r * r
    sums_ref[...] = block_of([column_sum(square), column_sum(square * half_of(energy_ref, side))])
    base_ref[...] = columns_product(t_parts_ref, side, two_parts(r))


def project_send(own_ref, t_parts_ref, energy_ref, base_ref, sums_ref, fixed_ref, alpha_ref, y_ref, r_ref, v_ref, send_ref, rhs_ref, tail_ref, next_ref, unit_ref, *, chips):
    side = 1 - own_ref[LEAD]
    r, unit_ref[...] = advance_other(own_ref, energy_ref, fixed_ref, alpha_ref, y_ref, r_ref, v_ref)
    next_ref[...] = r
    square = r * r
    squares = sums_ref[0:1, :] + column_sum(square)
    energies = sums_ref[1:2, :] + column_sum(square * half_of(energy_ref, side))
    tail = tail_of(own_ref, tail_ref.shape, squares, energies, chips)
    tail_ref[...] = tail
    rhs = two_parts(r)
    rhs_ref[...] = rhs
    part = t_parts_ref.shape[1] // 2
    add_product(t_parts_ref, side, rhs, base_ref, (1 - own_ref[CORE]) * part, send_ref, part)
    send_ref[part:, :] = tail


def project_keep(own_ref, t_parts_ref, base_ref, rhs_ref, tail_ref, keep_ref):
    part = t_parts_ref.shape[1] // 2
    side = 1 - own_ref[LEAD]
    add_product(t_parts_ref, side, rhs_ref[...], base_ref, own_ref[CORE] * part, keep_ref, part)
    keep_ref[part:, :] = tail_ref[...]


def exchange_own(own_ref, parts_ref, weights_ref, held_ref, base_ref, fixed_ref, *, chips):
    part = weights_ref.shape[0] // 2
    squares = column_sum(held_ref[part : part + chips, :])
    energies = column_sum(held_ref[part + chips : part + 2 * chips, :])
    beta = jnp.sqrt(squares + EPSILON)
    inverse = 1.0 / beta
    projected = held_ref[:part, :] * inverse
    weighted = half_of(weights_ref, own_ref[CORE]) * projected
    fixed_ref[...] = block_of(
        [beta, energies * inverse * inverse, column_sum(projected * weighted)]
    )
    base_ref[...] = columns_product(parts_ref, own_ref[CORE], two_parts(weighted))


def exchange_send(own_ref, parts_ref, weights_ref, base_ref, fixed_ref, other_ref, send_ref, rhs_ref, tail_ref):
    side = 1 - own_ref[CORE]
    projected = other_ref[...] * (1.0 / fixed_ref[0:1, :])
    weighted = half_of(weights_ref, side) * projected
    other = column_sum(projected * weighted)
    mine = fixed_ref[2:3, :]
    curvature = jnp.where(own_ref[CORE] == 0, mine + other, other + mine)
    row = lax.broadcasted_iota(jnp.int32, tail_ref.shape, 0)
    tail = jnp.where(row == own_ref[DEPTH], curvature, 0.0)
    tail_ref[...] = tail
    rhs = two_parts(weighted)
    rhs_ref[...] = rhs
    part = parts_ref.shape[1] // 2
    add_product(parts_ref, side, rhs, base_ref, (1 - own_ref[LEAD]) * part, send_ref, part)
    send_ref[part:, :] = tail


def exchange_keep(own_ref, parts_ref, base_ref, rhs_ref, tail_ref, keep_ref):
    part = parts_ref.shape[1] // 2
    side = 1 - own_ref[CORE]
    add_product(parts_ref, side, rhs_ref[...], base_ref, own_ref[LEAD] * part, keep_ref, part)
    keep_ref[part:, :] = tail_ref[...]


def finish_own(own_ref, energy_ref, fixed_ref, y_ref, r_ref, v_ref, next_ref, square_ref, alpha_ref):
    r, _, alpha_ref[...] = advance_own(own_ref, energy_ref, fixed_ref, y_ref, r_ref, v_ref)
    next_ref[...] = r
    square_ref[...] = block_of([column_sum(r * r)])


def finish_other(own_ref, energy_ref, fixed_ref, alpha_ref, y_ref, r_ref, v_ref, own_half_ref, out_ref):
    side = own_ref[LEAD]
    part = own_half_ref.shape[0]
    other, _ = advance_other(own_ref, energy_ref, fixed_ref, alpha_ref, y_ref, r_ref, v_ref)
    out_ref[pl.ds(pl.multiple_of(side * part, ROWS), part), :] = own_half_ref[...]
    out_ref[pl.ds(pl.multiple_of((1 - side) * part, ROWS), part), :] = other


def swaps(size, bit):
    return [(i, i ^ bit) for i in range(size)]


def bits_of(size):
    return [1 << b for b in range(size.bit_length() - 1)]


def crossed_swaps(size):
    bits = bits_of(size)[1:]
    turned = bits[::-1]
    return [
        [(i, i ^ (turned[n] if i & 1 else bits[n])) for i in range(size)] for n in range(len(bits))
    ]


def depth_swaps(ka, ga):
    bits = bits_of(ga)
    orders = [bits, bits[1:2] + bits[:1] + bits[2:]]
    return [
        [(a * ga + g, a * ga + (g ^ orders[a & 1][n])) for a in range(ka) for g in range(ga)]
        for n in range(len(bits))
    ]


def chunks(size, cuts):
    edges = [0] + [size * c // 16 // ROWS * ROWS for c in cuts] + [None]
    return [slice(*pair) for pair in zip(edges[:-1], edges[1:])][::-1]


def size_of(at, size):
    return (size if at.stop is None else at.stop) - at.start


def joined(pieces):
    return [jnp.concatenate(part, axis=0) for part in zip(*pieces)]


def per_device(ka, ga, pair_densities, energies, coulomb, start):
    rows, cols = pair_densities.shape
    half_r, half_g = rows // 2, cols // 2
    chips = ka // 2
    s_rows = -(-2 * chips // ROWS) * ROWS
    z_rows = -(-ga // ROWS) * ROWS
    core, chip, depth = lax.axis_index("ka") & 1, lax.axis_index("ka") >> 1, lax.axis_index("ga")
    lead = jnp.where(core == 0, depth & 1, (depth >> 1) & 1)
    own = jnp.stack([core, lead, depth, chip]).astype(jnp.int32)
    parts, t_parts = pl.pallas_call(
        split_matrix,
        out_shape=[
            jax.ShapeDtypeStruct((2, rows, cols), B16),
            jax.ShapeDtypeStruct((2, cols, rows), B16),
        ],
        in_specs=[SMEM, pl.BlockSpec(memory_space=pltpu.HBM)],
        out_specs=[VMEM] * 2,
        scratch_shapes=[
            pltpu.VMEM((rows, cols), F32),
            pltpu.SemaphoreType.DMA((rows // min(half_r, 128),)),
        ],
        cost_estimate=pl.CostEstimate(flops=2**31, bytes_accessed=0, transcendentals=0),
        compiler_params=pltpu.CompilerParams(vmem_limit_bytes=34 * MIB),
    )(own, pair_densities)
    energy = jnp.broadcast_to(energies[:, None], (rows, LANES))
    weights = jnp.broadcast_to(coulomb[:, None], (cols, LANES))

    flops = rows * cols * LANES * 4
    edge = half_g * KA_CUT // 16 // LANES * LANES or LANES
    line, block, half = ((1, LANES), F32), ((ROWS, LANES), F32), ((half_r, LANES), F32)
    wide = 2 * LANES
    both = ("ka", "ga")
    first_round, *rounds = depth_swaps(ka, ga)

    alphas, betas = [], []
    r = v = fixed = y_own = y_other = None
    for step in range(ITERS):
        outs = [((half_g + s_rows, LANES), F32), ((half_r, wide), B16), ((s_rows, LANES), F32)]
        if step == 0:
            outs[1] = ((2, half_r, wide), B16)
            send, rhs, tail, *r = call(
                functools.partial(first_send, chips=chips),
                outs + [half, half],
                flops // 2,
                own,
                t_parts,
                energy,
                start,
            )
            v = (jnp.zeros_like(r[0]),) * 2
        else:
            base, sums, r_own, v_own, alpha = call(
                project_own,
                [((cols, LANES), F32), block, half, half, line],
                flops // 2,
                own,
                t_parts,
                energy,
                fixed,
                y_own,
                r[0],
                v[0],
            )
            send, rhs, tail, r_other, v_other = call(
                functools.partial(project_send, chips=chips),
                outs + [half, half],
                flops // 4,
                own,
                t_parts,
                energy,
                base,
                sums,
                fixed,
                alpha,
                y_other,
                r[1],
                v[1],
            )
            r, v = (r_own, r_other), (v_own, v_other)
            alphas.append(alpha)
        arrived = lax.ppermute(send, "ka", swaps(ka, 1))
        if step == 0:
            (keep,) = call(first_keep, outs[:1], flops // 2, own, t_parts, rhs, tail)
        else:
            (keep,) = call(project_keep, outs[:1], flops // 4, own, t_parts, base, rhs, tail)
        pieces = []
        for at in (slice(edge, None), slice(0, edge)):
            held = keep[at] + arrived[at]
            for pairs in crossed_swaps(ka):
                held = held + lax.ppermute(held, "ka", pairs)
            pieces.insert(0, (held, lax.ppermute(held[: size_of(at, half_g)], "ka", swaps(ka, 1))))
        held, other = joined(pieces)
        base, fixed = call(
            functools.partial(exchange_own, chips=chips),
            [((rows, LANES), F32), block],
            flops // 2,
            own,
            parts,
            weights,
            held,
        )
        if step > 0:
            betas.append(fixed[0:1])
        outs = [((half_r + z_rows, LANES), F32), ((half_g, wide), B16), ((z_rows, LANES), F32)]
        send, rhs, tail = call(exchange_send, outs, flops // 4, own, parts, weights, base, fixed, other)
        pieces = []
        arrived = [
            lax.ppermute(send[at], both, first_round) for at in chunks(half_r, GA_CUTS)
        ]
        (keep,) = call(exchange_keep, outs[:1], flops // 4, own, parts, base, rhs, tail)
        for at, part in zip(chunks(half_r, GA_CUTS), arrived):
            y_own = keep[at] + part
            for pairs in rounds:
                y_own = y_own + lax.ppermute(y_own, both, pairs)
            y_part = y_own[: size_of(at, half_r)]
            y_part = lax.ppermute(y_part, both, first_round)
            pieces.insert(0, (y_own, y_part))
        y_own, y_other = joined(pieces)
    r_own, square, alpha = call(finish_own, [half, block, line], 2**20, own, energy, fixed, y_own, r[0], v[0])
    alphas.append(alpha)
    came = lax.ppermute(square, both, first_round)
    square = square + came
    for bit in bits_of(ka):
        came = lax.ppermute(square, "ka", swaps(ka, bit))
        square = square + came
    (last,) = call(
        finish_other,
        [((rows, LANES), F32)],
        flops // 4,
        own,
        energy,
        fixed,
        alpha,
        y_other,
        r[1],
        v[1],
        r_own,
    )
    beta = jnp.sqrt(square[0:1] + EPSILON)
    betas.append(beta)
    return (
        jnp.concatenate(alphas, axis=0),
        jnp.concatenate(betas, axis=0),
        last / beta,
    )


def solution(mesh):
    placed = (P("ka", "ga"), P("ka"), P("ga"), P("ka", None))
    return jax.shard_map(
        functools.partial(per_device, mesh.shape["ka"], mesh.shape["ga"]),
        mesh=mesh,
        in_specs=placed,
        out_specs=(P(), P(), P("ka", None)),
        check_vma=False,
    )
```

profile of v0, /device:TPU:0, one launch (start us, length us, event | category | flops | bytes accessed | tf_op | source)
XLA Modules:
  0.0 211.5 jit_solution(18157311498126808530)
XLA Ops:
  0.7 4.8 %shard_map.67 = (bf16[2,1024,2048]{2,1,0:T(8,128)(2,1)S(1)}, bf16[2,2048,1024]{2,1,0:T(8,128)(2,1)S(1)}) custom-call(s32[4]{0:T(128)S(1)} %pad_add_fusion.own_ref, f32[1024,2048]{1,0:T(8,128)} %m_ref.1), custom_call_target="tpu_custom_call" | custom-call | flops 2147483648 | tf_op jit(solution)/shard_map/pallas_call | solution.py:295
  5.8 1.9 shard_map.68
  10.1 2.6 %collective-permute-start.3 = (f32[648,128]{1,0:T(8,128)S(1)}, f32[648,128]{1,0:T(8,128)S(1)}, u32[]{:S(2)}, u32[]{:S(2)}) collective-permute-start(f32[648,128]{1,0:T(8,128)S(1)} %slice_add_fusion.3), channel_id=1, source_target_pairs={{0,8},{4,20},{8,0},{12,28},{16,24},{20,4},{24,16},{28,12},{1,9},{5... | collective-permute-start | bytes 995336 | tf_op jit(solution)/shard_map/ppermute | solution.py:375
  12.8 5.0 %collective-permute-done.3 = f32[648,128]{1,0:T(8,128)S(1)} collective-permute-done((f32[648,128]{1,0:T(8,128)S(1)}, f32[648,128]{1,0:T(8,128)S(1)}, u32[]{:S(2)}, u32[]{:S(2)}) %collective-permute-start.3) | collective-permute-done | bytes 331808 | tf_op jit(solution)/shard_map/ppermute | solution.py:375
  17.8 2.1 collective-permute-start.4
  20.0 2.1 collective-permute-start.2
  22.1 3.0 %collective-permute-done.4 = f32[648,128]{1,0:T(8,128)S(1)} collective-permute-done((f32[648,128]{1,0:T(8,128)S(1)}, f32[648,128]{1,0:T(8,128)S(1)}, u32[]{:S(2)}, u32[]{:S(2)}) %collective-permute-start.4) | collective-permute-done | bytes 331808 | tf_op jit(solution)/shard_map/ppermute | solution.py:375
  25.2 2.0 collective-permute-done.2
  30.9 2.1 %collective-permute-start.9 = (f32[264,128]{1,0:T(8,128)S(1)}, f32[264,128]{1,0:T(8,128)S(1)}, u32[]{:S(2)}, u32[]{:S(2)}) collective-permute-start(f32[264,128]{1,0:T(8,128)S(1)} %slice.140), channel_id=1, source_target_pairs={{0,1},{1,0},{2,3},{3,2},{4,6},{5,7},{6,4},{7,5},{8,9},{9,8},{10,11... | collective-permute-start | bytes 405512 | tf_op jit(solution)/shard_map/ppermute | solution.py:393
  34.3 2.8 %collective-permute-done.9 = f32[264,128]{1,0:T(8,128)S(1)} collective-permute-done((f32[264,128]{1,0:T(8,128)S(1)}, f32[264,128]{1,0:T(8,128)S(1)}, u32[]{:S(2)}, u32[]{:S(2)}) %collective-permute-start.9) | collective-permute-done | bytes 135200 | tf_op jit(solution)/shard_map/ppermute | solution.py:393
  37.1 3.3 %collective-permute-start.10 = (f32[264,128]{1,0:T(8,128)S(1)}, f32[264,128]{1,0:T(8,128)S(1)}, u32[]{:S(2)}, u32[]{:S(2)}) collective-permute-start(f32[264,128]{1,0:T(8,128)S(1)} %slice_add_fusion.11), channel_id=1, source_target_pairs={{0,2},{1,3},{2,0},{3,1},{4,5},{5,4},{6,7},{7,6},{8,10},{9,11},{10,... | collective-permute-start | bytes 405512 | tf_op jit(solution)/shard_map/ppermute | solution.py:399
  40.5 2.3 %collective-permute-start.8 = (f32[256,128]{1,0:T(8,128)S(1)}, f32[256,128]{1,0:T(8,128)S(1)}, u32[]{:S(2)}, u32[]{:S(2)}) collective-permute-start(f32[256,128]{1,0:T(8,128)S(1)} %slice_add_fusion.15), channel_id=1, source_target_pairs={{0,2},{1,3},{2,0},{3,1},{4,5},{5,4},{6,7},{7,6},{8,10},{9,11},{10,... | collective-permute-start | bytes 393224 | tf_op jit(solution)/shard_map/ppermute | solution.py:399
  42.8 5.1 %collective-permute-done.8 = f32[256,128]{1,0:T(8,128)S(1)} collective-permute-done((f32[256,128]{1,0:T(8,128)S(1)}, f32[256,128]{1,0:T(8,128)S(1)}, u32[]{:S(2)}, u32[]{:S(2)}) %collective-permute-start.8) | collective-permute-done | bytes 131104 | tf_op jit(solution)/shard_map/ppermute | solution.py:399
  50.1 1.9 shard_map.73
  52.0 2.5 %collective-permute-done.11 = f32[256,128]{1,0:T(8,128)S(1)} collective-permute-done((f32[256,128]{1,0:T(8,128)S(1)}, f32[256,128]{1,0:T(8,128)S(1)}, u32[]{:S(2)}, u32[]{:S(2)}) %collective-permute-start.11) | collective-permute-done | bytes 131104 | tf_op jit(solution)/shard_map/ppermute | solution.py:401
  54.5 1.9 collective-permute-done.12
  59.8 1.9 collective-permute-start.16
  62.0 5.0 %collective-permute-done.16 = f32[648,128]{1,0:T(8,128)S(1)} collective-permute-done((f32[648,128]{1,0:T(8,128)S(1)}, f32[648,128]{1,0:T(8,128)S(1)}, u32[]{:S(2)}, u32[]{:S(2)}) %collective-permute-start.16) | collective-permute-done | bytes 331808 | tf_op jit(solution)/shard_map/ppermute | solution.py:375
  67.0 1.9 collective-permute-start.17
  69.1 2.0 collective-permute-start.15
  71.1 3.1 %collective-permute-done.17 = f32[648,128]{1,0:T(8,128)S(1)} collective-permute-done((f32[648,128]{1,0:T(8,128)S(1)}, f32[648,128]{1,0:T(8,128)S(1)}, u32[]{:S(2)}, u32[]{:S(2)}) %collective-permute-start.17) | collective-permute-done | bytes 331808 | tf_op jit(solution)/shard_map/ppermute | solution.py:375
  74.3 1.9 collective-permute-done.15
  76.4 2.0 shard_map.76
  83.2 3.4 %collective-permute-done.22 = f32[264,128]{1,0:T(8,128)S(1)} collective-permute-done((f32[264,128]{1,0:T(8,128)S(1)}, f32[264,128]{1,0:T(8,128)S(1)}, u32[]{:S(2)}, u32[]{:S(2)}) %collective-permute-start.22) | collective-permute-done | bytes 135200 | tf_op jit(solution)/shard_map/ppermute | solution.py:393
  86.7 2.0 collective-permute-start.23
  89.4 1.9 collective-permute-start.21
  91.3 5.2 %collective-permute-done.21 = f32[256,128]{1,0:T(8,128)S(1)} collective-permute-done((f32[256,128]{1,0:T(8,128)S(1)}, f32[256,128]{1,0:T(8,128)S(1)}, u32[]{:S(2)}, u32[]{:S(2)}) %collective-permute-start.21) | collective-permute-done | bytes 131104 | tf_op jit(solution)/shard_map/ppermute | solution.py:399
  98.7 1.9 shard_map.79
  100.6 2.9 %collective-permute-done.24 = f32[256,128]{1,0:T(8,128)S(1)} collective-permute-done((f32[256,128]{1,0:T(8,128)S(1)}, f32[256,128]{1,0:T(8,128)S(1)}, u32[]{:S(2)}, u32[]{:S(2)}) %collective-permute-start.24) | collective-permute-done | bytes 131104 | tf_op jit(solution)/shard_map/ppermute | solution.py:401
  110.8 5.0 %collective-permute-done.29 = f32[648,128]{1,0:T(8,128)S(1)} collective-permute-done((f32[648,128]{1,0:T(8,128)S(1)}, f32[648,128]{1,0:T(8,128)S(1)}, u32[]{:S(2)}, u32[]{:S(2)}) %collective-permute-start.29) | collective-permute-done | bytes 331808 | tf_op jit(solution)/shard_map/ppermute | solution.py:375
  115.8 2.0 collective-permute-start.30
  117.9 2.1 collective-permute-start.28
  120.0 3.0 %collective-permute-done.30 = f32[648,128]{1,0:T(8,128)S(1)} collective-permute-done((f32[648,128]{1,0:T(8,128)S(1)}, f32[648,128]{1,0:T(8,128)S(1)}, u32[]{:S(2)}, u32[]{:S(2)}) %collective-permute-start.30) | collective-permute-done | bytes 331808 | tf_op jit(solution)/shard_map/ppermute | solution.py:375
  123.1 2.0 collective-permute-done.28
  131.9 3.4 %collective-permute-done.35 = f32[264,128]{1,0:T(8,128)S(1)} collective-permute-done((f32[264,128]{1,0:T(8,128)S(1)}, f32[264,128]{1,0:T(8,128)S(1)}, u32[]{:S(2)}, u32[]{:S(2)}) %collective-permute-start.35) | collective-permute-done | bytes 135200 | tf_op jit(solution)/shard_map/ppermute | solution.py:393
  139.7 5.8 %collective-permute-done.34 = f32[256,128]{1,0:T(8,128)S(1)} collective-permute-done((f32[256,128]{1,0:T(8,128)S(1)}, f32[256,128]{1,0:T(8,128)S(1)}, u32[]{:S(2)}, u32[]{:S(2)}) %collective-permute-start.34) | collective-permute-done | bytes 131104 | tf_op jit(solution)/shard_map/ppermute | solution.py:399
  147.7 1.9 shard_map.85
  149.6 2.9 %collective-permute-done.37 = f32[256,128]{1,0:T(8,128)S(1)} collective-permute-done((f32[256,128]{1,0:T(8,128)S(1)}, f32[256,128]{1,0:T(8,128)S(1)}, u32[]{:S(2)}, u32[]{:S(2)}) %collective-permute-start.37) | collective-permute-done | bytes 131104 | tf_op jit(solution)/shard_map/ppermute | solution.py:401
  159.4 5.0 %collective-permute-done.42 = f32[648,128]{1,0:T(8,128)S(1)} collective-permute-done((f32[648,128]{1,0:T(8,128)S(1)}, f32[648,128]{1,0:T(8,128)S(1)}, u32[]{:S(2)}, u32[]{:S(2)}) %collective-permute-start.42) | collective-permute-done | bytes 331808 | tf_op jit(solution)/shard_map/ppermute | solution.py:375
  164.5 2.0 collective-permute-start.43
  166.6 2.2 %collective-permute-start.41 = (f32[384,128]{1,0:T(8,128)S(1)}, f32[384,128]{1,0:T(8,128)S(1)}, u32[]{:S(2)}, u32[]{:S(2)}) collective-permute-start(f32[384,128]{1,0:T(8,128)S(1)} %add.169), channel_id=1, source_target_pairs={{0,16},{4,12},{8,24},{12,4},{16,0},{20,28},{24,8},{28,20},{1,17},{... | collective-permute-start | bytes 589832 | tf_op jit(solution)/shard_map/ppermute | solution.py:375
  168.7 2.9 %collective-permute-done.43 = f32[648,128]{1,0:T(8,128)S(1)} collective-permute-done((f32[648,128]{1,0:T(8,128)S(1)}, f32[648,128]{1,0:T(8,128)S(1)}, u32[]{:S(2)}, u32[]{:S(2)}) %collective-permute-start.43) | collective-permute-done | bytes 331808 | tf_op jit(solution)/shard_map/ppermute | solution.py:375
  171.8 2.0 collective-permute-done.41
  180.5 3.1 %collective-permute-done.48 = f32[264,128]{1,0:T(8,128)S(1)} collective-permute-done((f32[264,128]{1,0:T(8,128)S(1)}, f32[264,128]{1,0:T(8,128)S(1)}, u32[]{:S(2)}, u32[]{:S(2)}) %collective-permute-start.48) | collective-permute-done | bytes 135200 | tf_op jit(solution)/shard_map/ppermute | solution.py:393
  183.6 1.9 collective-permute-start.49
  188.1 5.8 %collective-permute-done.47 = f32[256,128]{1,0:T(8,128)S(1)} collective-permute-done((f32[256,128]{1,0:T(8,128)S(1)}, f32[256,128]{1,0:T(8,128)S(1)}, u32[]{:S(2)}, u32[]{:S(2)}) %collective-permute-start.47) | collective-permute-done | bytes 131104 | tf_op jit(solution)/shard_map/ppermute | solution.py:399
  195.2 3.1 %collective-permute-done.50 = f32[8,128]{1,0:T(8,128)S(1)} collective-permute-done((f32[8,128]{1,0:T(8,128)S(1)}, f32[8,128]{1,0:T(8,128)S(1)}, u32[]{:S(2)}, u32[]{:S(2)}) %collective-permute-start.50) | collective-permute-done | bytes 4128 | tf_op jit(solution)/shard_map/ppermute | solution.py:406
  207.3 2.7 %collective-permute-done.55 = f32[256,128]{1,0:T(8,128)S(1)} collective-permute-done((f32[256,128]{1,0:T(8,128)S(1)}, f32[256,128]{1,0:T(8,128)S(1)}, u32[]{:S(2)}, u32[]{:S(2)}) %collective-permute-start.55) | collective-permute-done | bytes 131104 | tf_op jit(solution)/shard_map/ppermute | solution.py:401
  (183 shorter events, 71.3 us)
Async XLA Ops:
  7.6 2.4 %collective-permute-start = (f32[1032,128]{1,0:T(8,128)S(1)}, f32[1032,128]{1,0:T(8,128)S(1)}, u32[]{:S(2)}, u32[]{:S(2)}) collective-permute-start(f32[1032,128]{1,0:T(8,128)S(1)} %get-tuple-element.67), channel_id=1, source_target_pairs={{0,4},{4,0},{8,12},{12,8},{16,20},{20,16},{24,28},{28,24},{1,5},{5... | collective-permute-start | bytes 1585160 | tf_op jit(solution)/shard_map/ppermute | solution.py:366
  10.1 7.7 %collective-permute-start.3 = (f32[648,128]{1,0:T(8,128)S(1)}, f32[648,128]{1,0:T(8,128)S(1)}, u32[]{:S(2)}, u32[]{:S(2)}) collective-permute-start(f32[648,128]{1,0:T(8,128)S(1)} %slice_add_fusion.3), channel_id=1, source_target_pairs={{0,8},{4,20},{8,0},{12,28},{16,24},{20,4},{24,16},{28,12},{1,9},{5... | collective-permute-start | bytes 995336 | tf_op jit(solution)/shard_map/ppermute | solution.py:375
  12.7 7.2 %collective-permute-start.1 = (f32[384,128]{1,0:T(8,128)S(1)}, f32[384,128]{1,0:T(8,128)S(1)}, u32[]{:S(2)}, u32[]{:S(2)}) collective-permute-start(f32[384,128]{1,0:T(8,128)S(1)} %slice_add_fusion.7), channel_id=1, source_target_pairs={{0,8},{4,20},{8,0},{12,28},{16,24},{20,4},{24,16},{28,12},{1,9},{5... | collective-permute-start | bytes 589832 | tf_op jit(solution)/shard_map/ppermute | solution.py:375
  17.8 7.2 %collective-permute-start.4 = (f32[648,128]{1,0:T(8,128)S(1)}, f32[648,128]{1,0:T(8,128)S(1)}, u32[]{:S(2)}, u32[]{:S(2)}) collective-permute-start(f32[648,128]{1,0:T(8,128)S(1)} %add.142), channel_id=1, source_target_pairs={{0,16},{4,12},{8,24},{12,4},{16,0},{20,28},{24,8},{28,20},{1,17},{... | collective-permute-start | bytes 995336 | tf_op jit(solution)/shard_map/ppermute | solution.py:375
  20.0 7.2 %collective-permute-start.2 = (f32[384,128]{1,0:T(8,128)S(1)}, f32[384,128]{1,0:T(8,128)S(1)}, u32[]{:S(2)}, u32[]{:S(2)}) collective-permute-start(f32[384,128]{1,0:T(8,128)S(1)} %add.139), channel_id=1, source_target_pairs={{0,16},{4,12},{8,24},{12,4},{16,0},{20,28},{24,8},{28,20},{1,17},{... | collective-permute-start | bytes 589832 | tf_op jit(solution)/shard_map/ppermute | solution.py:375
  25.1 4.4 %collective-permute-start.6 = (f32[640,128]{1,0:T(8,128)S(1)}, f32[640,128]{1,0:T(8,128)S(1)}, u32[]{:S(2)}, u32[]{:S(2)}) collective-permute-start(f32[640,128]{1,0:T(8,128)S(1)} %slice.180), channel_id=1, source_target_pairs={{0,4},{4,0},{8,12},{12,8},{16,20},{20,16},{24,28},{28,24},{1,5},{5... | collective-permute-start | bytes 983048 | tf_op jit(solution)/shard_map/ppermute | solution.py:376
  30.9 6.2 %collective-permute-start.9 = (f32[264,128]{1,0:T(8,128)S(1)}, f32[264,128]{1,0:T(8,128)S(1)}, u32[]{:S(2)}, u32[]{:S(2)}) collective-permute-start(f32[264,128]{1,0:T(8,128)S(1)} %slice.140), channel_id=1, source_target_pairs={{0,1},{1,0},{2,3},{3,2},{4,6},{5,7},{6,4},{7,5},{8,9},{9,8},{10,11... | collective-permute-start | bytes 405512 | tf_op jit(solution)/shard_map/ppermute | solution.py:393
  33.0 7.5 %collective-permute-start.7 = (f32[256,128]{1,0:T(8,128)S(1)}, f32[256,128]{1,0:T(8,128)S(1)}, u32[]{:S(2)}, u32[]{:S(2)}) collective-permute-start(f32[256,128]{1,0:T(8,128)S(1)} %slice.138), channel_id=1, source_target_pairs={{0,1},{1,0},{2,3},{3,2},{4,6},{5,7},{6,4},{7,5},{8,9},{9,8},{10,11... | collective-permute-start | bytes 393224 | tf_op jit(solution)/shard_map/ppermute | solution.py:393
  37.1 12.1 %collective-permute-start.10 = (f32[264,128]{1,0:T(8,128)S(1)}, f32[264,128]{1,0:T(8,128)S(1)}, u32[]{:S(2)}, u32[]{:S(2)}) collective-permute-start(f32[264,128]{1,0:T(8,128)S(1)} %slice_add_fusion.11), channel_id=1, source_target_pairs={{0,2},{1,3},{2,0},{3,1},{4,5},{5,4},{6,7},{7,6},{8,10},{9,11},{10,... | collective-permute-start | bytes 405512 | tf_op jit(solution)/shard_map/ppermute | solution.py:399
  40.5 7.3 %collective-permute-start.8 = (f32[256,128]{1,0:T(8,128)S(1)}, f32[256,128]{1,0:T(8,128)S(1)}, u32[]{:S(2)}, u32[]{:S(2)}) collective-permute-start(f32[256,128]{1,0:T(8,128)S(1)} %slice_add_fusion.15), channel_id=1, source_target_pairs={{0,2},{1,3},{2,0},{3,1},{4,5},{5,4},{6,7},{7,6},{8,10},{9,11},{10,... | collective-permute-start | bytes 393224 | tf_op jit(solution)/shard_map/ppermute | solution.py:399
  47.8 6.6 %collective-permute-start.11 = (f32[256,128]{1,0:T(8,128)S(1)}, f32[256,128]{1,0:T(8,128)S(1)}, u32[]{:S(2)}, u32[]{:S(2)}) collective-permute-start(f32[256,128]{1,0:T(8,128)S(1)} %add.145), channel_id=1, source_target_pairs={{0,1},{1,0},{2,3},{3,2},{4,6},{5,7},{6,4},{7,5},{8,9},{9,8},{10,11... | collective-permute-start | bytes 393224 | tf_op jit(solution)/shard_map/ppermute | solution.py:401
  49.2 7.2 %collective-permute-start.12 = (f32[256,128]{1,0:T(8,128)S(1)}, f32[256,128]{1,0:T(8,128)S(1)}, u32[]{:S(2)}, u32[]{:S(2)}) collective-permute-start(f32[256,128]{1,0:T(8,128)S(1)} %slice.183), channel_id=1, source_target_pairs={{0,1},{1,0},{2,3},{3,2},{4,6},{5,7},{6,4},{7,5},{8,9},{9,8},{10,11... | collective-permute-start | bytes 393224 | tf_op jit(solution)/shard_map/ppermute | solution.py:401
  59.8 7.2 %collective-permute-start.16 = (f32[648,128]{1,0:T(8,128)S(1)}, f32[648,128]{1,0:T(8,128)S(1)}, u32[]{:S(2)}, u32[]{:S(2)}) collective-permute-start(f32[648,128]{1,0:T(8,128)S(1)} %slice_add_fusion.2), channel_id=1, source_target_pairs={{0,8},{4,20},{8,0},{12,28},{16,24},{20,4},{24,16},{28,12},{1,9},{5... | collective-permute-start | bytes 995336 | tf_op jit(solution)/shard_map/ppermute | solution.py:375
  61.7 7.4 %collective-permute-start.14 = (f32[384,128]{1,0:T(8,128)S(1)}, f32[384,128]{1,0:T(8,128)S(1)}, u32[]{:S(2)}, u32[]{:S(2)}) collective-permute-start(f32[384,128]{1,0:T(8,128)S(1)} %slice_add_fusion.6), channel_id=1, source_target_pairs={{0,8},{4,20},{8,0},{12,28},{16,24},{20,4},{24,16},{28,12},{1,9},{5... | collective-permute-start | bytes 589832 | tf_op jit(solution)/shard_map/ppermute | solution.py:375
  67.0 7.2 %collective-permute-start.17 = (f32[648,128]{1,0:T(8,128)S(1)}, f32[648,128]{1,0:T(8,128)S(1)}, u32[]{:S(2)}, u32[]{:S(2)}) collective-permute-start(f32[648,128]{1,0:T(8,128)S(1)} %add.152), channel_id=1, source_target_pairs={{0,16},{4,12},{8,24},{12,4},{16,0},{20,28},{24,8},{28,20},{1,17},{... | collective-permute-start | bytes 995336 | tf_op jit(solution)/shard_map/ppermute | solution.py:375
  69.1 7.2 %collective-permute-start.15 = (f32[384,128]{1,0:T(8,128)S(1)}, f32[384,128]{1,0:T(8,128)S(1)}, u32[]{:S(2)}, u32[]{:S(2)}) collective-permute-start(f32[384,128]{1,0:T(8,128)S(1)} %add.149), channel_id=1, source_target_pairs={{0,16},{4,12},{8,24},{12,4},{16,0},{20,28},{24,8},{28,20},{1,17},{... | collective-permute-start | bytes 589832 | tf_op jit(solution)/shard_map/ppermute | solution.py:375
  74.3 4.2 %collective-permute-start.19 = (f32[640,128]{1,0:T(8,128)S(1)}, f32[640,128]{1,0:T(8,128)S(1)}, u32[]{:S(2)}, u32[]{:S(2)}) collective-permute-start(f32[640,128]{1,0:T(8,128)S(1)} %slice.188), channel_id=1, source_target_pairs={{0,4},{4,0},{8,12},{12,8},{16,20},{20,16},{24,28},{28,24},{1,5},{5... | collective-permute-start | bytes 983048 | tf_op jit(solution)/shard_map/ppermute | solution.py:376
  79.8 6.8 %collective-permute-start.22 = (f32[264,128]{1,0:T(8,128)S(1)}, f32[264,128]{1,0:T(8,128)S(1)}, u32[]{:S(2)}, u32[]{:S(2)}) collective-permute-start(f32[264,128]{1,0:T(8,128)S(1)} %slice.150), channel_id=1, source_target_pairs={{0,1},{1,0},{2,3},{3,2},{4,6},{5,7},{6,4},{7,5},{8,9},{9,8},{10,11... | collective-permute-start | bytes 405512 | tf_op jit(solution)/shard_map/ppermute | solution.py:393
  81.0 8.4 %collective-permute-start.20 = (f32[256,128]{1,0:T(8,128)S(1)}, f32[256,128]{1,0:T(8,128)S(1)}, u32[]{:S(2)}, u32[]{:S(2)}) collective-permute-start(f32[256,128]{1,0:T(8,128)S(1)} %slice.148), channel_id=1, source_target_pairs={{0,1},{1,0},{2,3},{3,2},{4,6},{5,7},{6,4},{7,5},{8,9},{9,8},{10,11... | collective-permute-start | bytes 393224 | tf_op jit(solution)/shard_map/ppermute | solution.py:393
  86.7 10.9 %collective-permute-start.23 = (f32[264,128]{1,0:T(8,128)S(1)}, f32[264,128]{1,0:T(8,128)S(1)}, u32[]{:S(2)}, u32[]{:S(2)}) collective-permute-start(f32[264,128]{1,0:T(8,128)S(1)} %slice_add_fusion.10), channel_id=1, source_target_pairs={{0,2},{1,3},{2,0},{3,1},{4,5},{5,4},{6,7},{7,6},{8,10},{9,11},{10,... | collective-permute-start | bytes 405512 | tf_op jit(solution)/shard_map/ppermute | solution.py:399
  89.4 7.1 %collective-permute-start.21 = (f32[256,128]{1,0:T(8,128)S(1)}, f32[256,128]{1,0:T(8,128)S(1)}, u32[]{:S(2)}, u32[]{:S(2)}) collective-permute-start(f32[256,128]{1,0:T(8,128)S(1)} %slice_add_fusion.14), channel_id=1, source_target_pairs={{0,2},{1,3},{2,0},{3,1},{4,5},{5,4},{6,7},{7,6},{8,10},{9,11},{10,... | collective-permute-start | bytes 393224 | tf_op jit(solution)/shard_map/ppermute | solution.py:399
  96.5 7.0 %collective-permute-start.24 = (f32[256,128]{1,0:T(8,128)S(1)}, f32[256,128]{1,0:T(8,128)S(1)}, u32[]{:S(2)}, u32[]{:S(2)}) collective-permute-start(f32[256,128]{1,0:T(8,128)S(1)} %add.155), channel_id=1, source_target_pairs={{0,1},{1,0},{2,3},{3,2},{4,6},{5,7},{6,4},{7,5},{8,9},{9,8},{10,11... | collective-permute-start | bytes 393224 | tf_op jit(solution)/shard_map/ppermute | solution.py:401
  97.6 7.6 %collective-permute-start.25 = (f32[256,128]{1,0:T(8,128)S(1)}, f32[256,128]{1,0:T(8,128)S(1)}, u32[]{:S(2)}, u32[]{:S(2)}) collective-permute-start(f32[256,128]{1,0:T(8,128)S(1)} %slice.191), channel_id=1, source_target_pairs={{0,1},{1,0},{2,3},{3,2},{4,6},{5,7},{6,4},{7,5},{8,9},{9,8},{10,11... | collective-permute-start | bytes 393224 | tf_op jit(solution)/shard_map/ppermute | solution.py:401
  108.6 7.2 %collective-permute-start.29 = (f32[648,128]{1,0:T(8,128)S(1)}, f32[648,128]{1,0:T(8,128)S(1)}, u32[]{:S(2)}, u32[]{:S(2)}) collective-permute-start(f32[648,128]{1,0:T(8,128)S(1)} %slice_add_fusion.1), channel_id=1, source_target_pairs={{0,8},{4,20},{8,0},{12,28},{16,24},{20,4},{24,16},{28,12},{1,9},{5... | collective-permute-start | bytes 995336 | tf_op jit(solution)/shard_map/ppermute | solution.py:375
  110.4 7.5 %collective-permute-start.27 = (f32[384,128]{1,0:T(8,128)S(1)}, f32[384,128]{1,0:T(8,128)S(1)}, u32[]{:S(2)}, u32[]{:S(2)}) collective-permute-start(f32[384,128]{1,0:T(8,128)S(1)} %slice_add_fusion.5), channel_id=1, source_target_pairs={{0,8},{4,20},{8,0},{12,28},{16,24},{20,4},{24,16},{28,12},{1,9},{5... | collective-permute-start | bytes 589832 | tf_op jit(solution)/shard_map/ppermute | solution.py:375
  115.8 7.2 %collective-permute-start.30 = (f32[648,128]{1,0:T(8,128)S(1)}, f32[648,128]{1,0:T(8,128)S(1)}, u32[]{:S(2)}, u32[]{:S(2)}) collective-permute-start(f32[648,128]{1,0:T(8,128)S(1)} %add.162), channel_id=1, source_target_pairs={{0,16},{4,12},{8,24},{12,4},{16,0},{20,28},{24,8},{28,20},{1,17},{... | collective-permute-start | bytes 995336 | tf_op jit(solution)/shard_map/ppermute | solution.py:375
  117.9 7.2 %collective-permute-start.28 = (f32[384,128]{1,0:T(8,128)S(1)}, f32[384,128]{1,0:T(8,128)S(1)}, u32[]{:S(2)}, u32[]{:S(2)}) collective-permute-start(f32[384,128]{1,0:T(8,128)S(1)} %add.159), channel_id=1, source_target_pairs={{0,16},{4,12},{8,24},{12,4},{16,0},{20,28},{24,8},{28,20},{1,17},{... | collective-permute-start | bytes 589832 | tf_op jit(solution)/shard_map/ppermute | solution.py:375
  123.1 4.0 %collective-permute-start.32 = (f32[640,128]{1,0:T(8,128)S(1)}, f32[640,128]{1,0:T(8,128)S(1)}, u32[]{:S(2)}, u32[]{:S(2)}) collective-permute-start(f32[640,128]{1,0:T(8,128)S(1)} %slice.196), channel_id=1, source_target_pairs={{0,4},{4,0},{8,12},{12,8},{16,20},{20,16},{24,28},{28,24},{1,5},{5... | collective-permute-start | bytes 983048 | tf_op jit(solution)/shard_map/ppermute | solution.py:376
  128.4 6.8 %collective-permute-start.35 = (f32[264,128]{1,0:T(8,128)S(1)}, f32[264,128]{1,0:T(8,128)S(1)}, u32[]{:S(2)}, u32[]{:S(2)}) collective-permute-start(f32[264,128]{1,0:T(8,128)S(1)} %slice.160), channel_id=1, source_target_pairs={{0,1},{1,0},{2,3},{3,2},{4,6},{5,7},{6,4},{7,5},{8,9},{9,8},{10,11... | collective-permute-start | bytes 405512 | tf_op jit(solution)/shard_map/ppermute | solution.py:393
  128.9 9.2 %collective-permute-start.33 = (f32[256,128]{1,0:T(8,128)S(1)}, f32[256,128]{1,0:T(8,128)S(1)}, u32[]{:S(2)}, u32[]{:S(2)}) collective-permute-start(f32[256,128]{1,0:T(8,128)S(1)} %slice.158), channel_id=1, source_target_pairs={{0,1},{1,0},{2,3},{3,2},{4,6},{5,7},{6,4},{7,5},{8,9},{9,8},{10,11... | collective-permute-start | bytes 393224 | tf_op jit(solution)/shard_map/ppermute | solution.py:393
  135.2 10.9 %collective-permute-start.36 = (f32[264,128]{1,0:T(8,128)S(1)}, f32[264,128]{1,0:T(8,128)S(1)}, u32[]{:S(2)}, u32[]{:S(2)}) collective-permute-start(f32[264,128]{1,0:T(8,128)S(1)} %slice_add_fusion.9), channel_id=1, source_target_pairs={{0,2},{1,3},{2,0},{3,1},{4,5},{5,4},{6,7},{7,6},{8,10},{9,11},{10,... | collective-permute-start | bytes 405512 | tf_op jit(solution)/shard_map/ppermute | solution.py:399
  138.1 7.3 %collective-permute-start.34 = (f32[256,128]{1,0:T(8,128)S(1)}, f32[256,128]{1,0:T(8,128)S(1)}, u32[]{:S(2)}, u32[]{:S(2)}) collective-permute-start(f32[256,128]{1,0:T(8,128)S(1)} %slice_add_fusion.13), channel_id=1, source_target_pairs={{0,2},{1,3},{2,0},{3,1},{4,5},{5,4},{6,7},{7,6},{8,10},{9,11},{10,... | collective-permute-start | bytes 393224 | tf_op jit(solution)/shard_map/ppermute | solution.py:399
  145.5 7.0 %collective-permute-start.37 = (f32[256,128]{1,0:T(8,128)S(1)}, f32[256,128]{1,0:T(8,128)S(1)}, u32[]{:S(2)}, u32[]{:S(2)}) collective-permute-start(f32[256,128]{1,0:T(8,128)S(1)} %add.165), channel_id=1, source_target_pairs={{0,1},{1,0},{2,3},{3,2},{4,6},{5,7},{6,4},{7,5},{8,9},{9,8},{10,11... | collective-permute-start | bytes 393224 | tf_op jit(solution)/shard_map/ppermute | solution.py:401
  146.1 7.7 %collective-permute-start.38 = (f32[256,128]{1,0:T(8,128)S(1)}, f32[256,128]{1,0:T(8,128)S(1)}, u32[]{:S(2)}, u32[]{:S(2)}) collective-permute-start(f32[256,128]{1,0:T(8,128)S(1)} %slice.199), channel_id=1, source_target_pairs={{0,1},{1,0},{2,3},{3,2},{4,6},{5,7},{6,4},{7,5},{8,9},{9,8},{10,11... | collective-permute-start | bytes 393224 | tf_op jit(solution)/shard_map/ppermute | solution.py:401
  157.2 7.2 %collective-permute-start.42 = (f32[648,128]{1,0:T(8,128)S(1)}, f32[648,128]{1,0:T(8,128)S(1)}, u32[]{:S(2)}, u32[]{:S(2)}) collective-permute-start(f32[648,128]{1,0:T(8,128)S(1)} %slice_add_fusion), channel_id=1, source_target_pairs={{0,8},{4,20},{8,0},{12,28},{16,24},{20,4},{24,16},{28,12},{1,9},{5... | collective-permute-start | bytes 995336 | tf_op jit(solution)/shard_map/ppermute | solution.py:375
  158.9 7.6 %collective-permute-start.40 = (f32[384,128]{1,0:T(8,128)S(1)}, f32[384,128]{1,0:T(8,128)S(1)}, u32[]{:S(2)}, u32[]{:S(2)}) collective-permute-start(f32[384,128]{1,0:T(8,128)S(1)} %slice_add_fusion.4), channel_id=1, source_target_pairs={{0,8},{4,20},{8,0},{12,28},{16,24},{20,4},{24,16},{28,12},{1,9},{5... | collective-permute-start | bytes 589832 | tf_op jit(solution)/shard_map/ppermute | solution.py:375
  164.5 7.2 %collective-permute-start.43 = (f32[648,128]{1,0:T(8,128)S(1)}, f32[648,128]{1,0:T(8,128)S(1)}, u32[]{:S(2)}, u32[]{:S(2)}) collective-permute-start(f32[648,128]{1,0:T(8,128)S(1)} %add.172), channel_id=1, source_target_pairs={{0,16},{4,12},{8,24},{12,4},{16,0},{20,28},{24,8},{28,20},{1,17},{... | collective-permute-start | bytes 995336 | tf_op jit(solution)/shard_map/ppermute | solution.py:375
  166.6 7.2 %collective-permute-start.41 = (f32[384,128]{1,0:T(8,128)S(1)}, f32[384,128]{1,0:T(8,128)S(1)}, u32[]{:S(2)}, u32[]{:S(2)}) collective-permute-start(f32[384,128]{1,0:T(8,128)S(1)} %add.169), channel_id=1, source_target_pairs={{0,16},{4,12},{8,24},{12,4},{16,0},{20,28},{24,8},{28,20},{1,17},{... | collective-permute-start | bytes 589832 | tf_op jit(solution)/shard_map/ppermute | solution.py:375
  171.7 4.0 %collective-permute-start.45 = (f32[640,128]{1,0:T(8,128)S(1)}, f32[640,128]{1,0:T(8,128)S(1)}, u32[]{:S(2)}, u32[]{:S(2)}) collective-permute-start(f32[640,128]{1,0:T(8,128)S(1)} %slice.204), channel_id=1, source_target_pairs={{0,4},{4,0},{8,12},{12,8},{16,20},{20,16},{24,28},{28,24},{1,5},{5... | collective-permute-start | bytes 983048 | tf_op jit(solution)/shard_map/ppermute | solution.py:376
  177.1 6.5 %collective-permute-start.48 = (f32[264,128]{1,0:T(8,128)S(1)}, f32[264,128]{1,0:T(8,128)S(1)}, u32[]{:S(2)}, u32[]{:S(2)}) collective-permute-start(f32[264,128]{1,0:T(8,128)S(1)} %slice.170), channel_id=1, source_target_pairs={{0,1},{1,0},{2,3},{3,2},{4,6},{5,7},{6,4},{7,5},{8,9},{9,8},{10,11... | collective-permute-start | bytes 405512 | tf_op jit(solution)/shard_map/ppermute | solution.py:393
  177.6 9.0 %collective-permute-start.46 = (f32[256,128]{1,0:T(8,128)S(1)}, f32[256,128]{1,0:T(8,128)S(1)}, u32[]{:S(2)}, u32[]{:S(2)}) collective-permute-start(f32[256,128]{1,0:T(8,128)S(1)} %slice.168), channel_id=1, source_target_pairs={{0,1},{1,0},{2,3},{3,2},{4,6},{5,7},{6,4},{7,5},{8,9},{9,8},{10,11... | collective-permute-start | bytes 393224 | tf_op jit(solution)/shard_map/ppermute | solution.py:393
  183.6 10.3 %collective-permute-start.49 = (f32[264,128]{1,0:T(8,128)S(1)}, f32[264,128]{1,0:T(8,128)S(1)}, u32[]{:S(2)}, u32[]{:S(2)}) collective-permute-start(f32[264,128]{1,0:T(8,128)S(1)} %slice_add_fusion.8), channel_id=1, source_target_pairs={{0,2},{1,3},{2,0},{3,1},{4,5},{5,4},{6,7},{7,6},{8,10},{9,11},{10,... | collective-permute-start | bytes 405512 | tf_op jit(solution)/shard_map/ppermute | solution.py:399
  186.6 7.3 %collective-permute-start.47 = (f32[256,128]{1,0:T(8,128)S(1)}, f32[256,128]{1,0:T(8,128)S(1)}, u32[]{:S(2)}, u32[]{:S(2)}) collective-permute-start(f32[256,128]{1,0:T(8,128)S(1)} %slice_add_fusion.12), channel_id=1, source_target_pairs={{0,2},{1,3},{2,0},{3,1},{4,5},{5,4},{6,7},{7,6},{8,10},{9,11},{10,... | collective-permute-start | bytes 393224 | tf_op jit(solution)/shard_map/ppermute | solution.py:399
  194.6 3.7 %collective-permute-start.50 = (f32[8,128]{1,0:T(8,128)S(1)}, f32[8,128]{1,0:T(8,128)S(1)}, u32[]{:S(2)}, u32[]{:S(2)}) collective-permute-start(f32[8,128]{1,0:T(8,128)S(1)} %get-tuple-element.119), channel_id=1, source_target_pairs={{0,1},{1,0},{2,3},{3,2},{4,6},{5,7},{6,4},{7,5},{8,9},{9,8},{10,11... | collective-permute-start | bytes 12296 | tf_op jit(solution)/shard_map/ppermute | solution.py:406
  199.5 3.6 %collective-permute-start.52 = (f32[8,128]{1,0:T(8,128)S(1)}, f32[8,128]{1,0:T(8,128)S(1)}, u32[]{:S(2)}, u32[]{:S(2)}) collective-permute-start(f32[8,128]{1,0:T(8,128)S(1)} %add.179), channel_id=1, source_target_pairs={{0,8},{4,12},{8,0},{12,4},{16,24},{20,28},{24,16},{28,20},{1,9},{5... | collective-permute-start | bytes 12296 | tf_op jit(solution)/shard_map/ppermute | solution.py:409
  201.0 6.3 %collective-permute-start.54 = (f32[256,128]{1,0:T(8,128)S(1)}, f32[256,128]{1,0:T(8,128)S(1)}, u32[]{:S(2)}, u32[]{:S(2)}) collective-permute-start(f32[256,128]{1,0:T(8,128)S(1)} %add.175), channel_id=1, source_target_pairs={{0,1},{1,0},{2,3},{3,2},{4,6},{5,7},{6,4},{7,5},{8,9},{9,8},{10,11... | collective-permute-start | bytes 393224 | tf_op jit(solution)/shard_map/ppermute | solution.py:401
  203.1 3.6 %collective-permute-start.53 = (f32[8,128]{1,0:T(8,128)S(1)}, f32[8,128]{1,0:T(8,128)S(1)}, u32[]{:S(2)}, u32[]{:S(2)}) collective-permute-start(f32[8,128]{1,0:T(8,128)S(1)} %add.180), channel_id=1, source_target_pairs={{0,16},{4,20},{8,24},{12,28},{16,0},{20,4},{24,8},{28,12},{1,17},{... | collective-permute-start | bytes 12296 | tf_op jit(solution)/shard_map/ppermute | solution.py:409
  204.7 5.3 %collective-permute-start.55 = (f32[256,128]{1,0:T(8,128)S(1)}, f32[256,128]{1,0:T(8,128)S(1)}, u32[]{:S(2)}, u32[]{:S(2)}) collective-permute-start(f32[256,128]{1,0:T(8,128)S(1)} %slice.207), channel_id=1, source_target_pairs={{0,1},{1,0},{2,3},{3,2},{4,6},{5,7},{6,4},{7,5},{8,9},{9,8},{10,11... | collective-permute-start | bytes 393224 | tf_op jit(solution)/shard_map/ppermute | solution.py:401
  (11 other events, 45.2 us)
where the time goes:
time: 212 us
  waiting for transfers between devices  102 us (48%)
  starting transfers between devices  62.9 us (30%)
  Pallas kernels  40.6 us (19%)
  other arithmetic  3.7 us (2%)
    ppermute x16, waiting for transfers between devices, per_device(): held = held + lax.ppermute(held, 'ka', pairs)  40.1 us
    pallas_call x25, Pallas kernels, call(): pl.pallas_call(body, out_shape=[jax.ShapeDtypeStruct(shape, dtype) for sh...  35.8 us
    ppermute x16, starting transfers between devices, per_device(): held = held + lax.ppermute(held, 'ka', pairs)  25.6 us
    ppermute x8, waiting for transfers between devices, per_device(): y_own = y_own + lax.ppermute(y_own, both, pairs)  21.9 us
    ppermute x8, starting transfers between devices, per_device(): y_own = y_own + lax.ppermute(y_own, both, pairs)  16.3 us
    ppermute x8, waiting for transfers between devices, per_device(): y_part = lax.ppermute(y_part, both, first_round)  16 us
    ppermute x8, waiting for transfers between devices, per_device(): lax.ppermute(send[at], both, first_round)  15.4 us
    ppermute x8, starting transfers between devices, per_device(): lax.ppermute(send[at], both, first_round)  8.69 us
  transfers between devices with their start and end apart: 56, of which 39 were waited for; matrix products, arithmetic and copies ran while one was open for 1% of the time, Pallas kernels for 11%

commit v1 on v0

--- a/solution.py
+++ b/solution.py
@@ -78,8 +78,16 @@
     return jnp.concatenate([hi, lo.astype(B16)], axis=1)
 
 
-def columns_product(parts_ref, side, rhs):
-    both = jnp.dot(parts_ref[side], jnp.concatenate([rhs, rhs], axis=0), preferred_element_type=F32)
+def columns_product(parts_ref, side, begin, rhs):
+    width = rhs.shape[0]
+    low = parts_ref.shape[2] // 2 + begin
+    if 2 * width == parts_ref.shape[2]:
+        matrix = parts_ref[side]
+    else:
+        matrix = jnp.concatenate(
+            [parts_ref[side, :, begin : begin + width], parts_ref[side, :, low : low + width]], axis=1
+        )
+    both = jnp.dot(matrix, jnp.concatenate([rhs, rhs], axis=0), preferred_element_type=F32)
     return both[:, :LANES] + both[:, LANES:]
 
 
@@ -167,7 +175,7 @@
 def project_rows(side, t_parts_ref, energy_ref, r, base_ref, sums_ref):
     square = r * r
     sums_ref[...] = block_of([column_sum(square), column_sum(square * half_of(energy_ref, side))])
-    base_ref[...] = columns_product(t_parts_ref, side, two_parts(r))
+    base_ref[...] = columns_product(t_parts_ref, side, 0, two_parts(r))
 
 
 def project_send(own_ref, t_parts_ref, energy_ref, base_ref, sums_ref, fixed_ref, alpha_ref, y_ref, r_ref, v_ref, send_ref, rhs_ref, tail_ref, next_ref, unit_ref, *, chips):
@@ -193,25 +201,39 @@
     keep_ref[part:, :] = tail_ref[...]
 
 
-def exchange_own(own_ref, parts_ref, weights_ref, held_ref, base_ref, fixed_ref, *, chips):
-    part = weights_ref.shape[0] // 2
+def weighted_rows(weights_ref, side, begin, projected):
+    at = side * (weights_ref.shape[0] // 2) + begin
+    return weights_ref[pl.ds(pl.multiple_of(at, ROWS), projected.shape[0]), :] * projected
+
+
+def exchange_first(own_ref, parts_ref, weights_ref, held_ref, base_ref, fixed_ref, *, chips, edge):
+    part = weights_ref.shape[0] // 2 - edge
     squares = column_sum(held_ref[part : part + chips, :])
     energies = column_sum(held_ref[part + chips : part + 2 * chips, :])
     beta = jnp.sqrt(squares + EPSILON)
     inverse = 1.0 / beta
     projected = held_ref[:part, :] * inverse
-    weighted = half_of(weights_ref, own_ref[CORE]) * projected
+    weighted = weighted_rows(weights_ref, own_ref[CORE], edge, projected)
     fixed_ref[...] = block_of(
         [beta, energies * inverse * inverse, column_sum(projected * weighted)]
     )
-    base_ref[...] = columns_product(parts_ref, own_ref[CORE], two_parts(weighted))
-
-
-def exchange_send(own_ref, parts_ref, weights_ref, base_ref, fixed_ref, other_ref, send_ref, rhs_ref, tail_ref):
+    base_ref[...] = columns_product(parts_ref, own_ref[CORE], edge, two_parts(weighted))
+
+
+def exchange_more(own_ref, parts_ref, weights_ref, held_ref, first_ref, sums_ref, base_ref, fixed_ref):
+    projected = held_ref[...] * (1.0 / sums_ref[0:1, :])
+    weighted = weighted_rows(weights_ref, own_ref[CORE], 0, projected)
+    total = sums_ref[2:3, :] + column_sum(projected * weighted)
+    fixed_ref[...] = block_of([sums_ref[0:1, :], sums_ref[1:2, :], total])
+    base_ref[...] = first_ref[...] + columns_product(parts_ref, own_ref[CORE], 0, two_parts(weighted))
+
+
+def exchange_send(own_ref, parts_ref, weights_ref, base_ref, fixed_ref, other_ref, send_ref, rhs_ref, tail_ref, *, edge):
     side = 1 - own_ref[CORE]
     projected = other_ref[...] * (1.0 / fixed_ref[0:1, :])
-    weighted = half_of(weights_ref, side) * projected
-    other = column_sum(projected * weighted)
+    weighted = weighted_rows(weights_ref, side, 0, projected)
+    terms = projected * weighted
+    other = column_sum(terms[edge:, :]) + column_sum(terms[:edge, :])
     mine = fixed_ref[2:3, :]
     curvature = jnp.where(own_ref[CORE] == 0, mine + other, other + mine)
     row = lax.broadcasted_iota(jnp.int32, tail_ref.shape, 0)
@@ -372,22 +394,28 @@
         for at in (slice(edge, None), slice(0, edge)):
             held = keep[at] + arrived[at]
             for pairs in crossed_swaps(ka):
-                held = held + lax.ppermute(held, "ka", pairs)
+                came = lax.ppermute(held, "ka", pairs)
+                held = held + came
             pieces.insert(0, (held, lax.ppermute(held[: size_of(at, half_g)], "ka", swaps(ka, 1))))
-        held, other = joined(pieces)
+        (held, head), (_, other) = pieces[1][:1] + pieces[0][:1], joined(pieces)
         base, fixed = call(
-            functools.partial(exchange_own, chips=chips),
+            functools.partial(exchange_first, chips=chips, edge=edge),
             [((rows, LANES), F32), block],
-            flops // 2,
+            flops // 4,
             own,
             parts,
             weights,
             held,
         )
+        base, fixed = call(
+            exchange_more, [((rows, LANES), F32), block], flops // 4, own, parts, weights, head, base, fixed
+        )
         if step > 0:
             betas.append(fixed[0:1])
         outs = [((half_r + z_rows, LANES), F32), ((half_g, wide), B16), ((z_rows, LANES), F32)]
-        send, rhs, tail = call(exchange_send, outs, flops // 4, own, parts, weights, base, fixed, other)
+        send, rhs, tail = call(
+            functools.partial(exchange_send, edge=edge), outs, flops // 4, own, parts, weights, base, fixed, other
+        )
         pieces = []
         arrived = [
             lax.ppermute(send[at], both, first_round) for at in chunks(half_r, GA_CUTS)

time: 212 us -> 231 us (1.090)
  waiting for transfers between devices: 102 us -> 116 us
  Pallas kernels: 40.6 us -> 43.9 us
  starting transfers between devices: 62.9 us -> 65.5 us
    ppermute x16, waiting for transfers between devices: 40.1 us -> 54 us  [per_device(): came = lax.ppermute(held, 'ka', pairs)]
    pallas_call x25 -> x29, Pallas kernels: 35.8 us -> 39.1 us  [call(): pl.pallas_call(body, out_shape=[jax.ShapeDtypeStruct(shape, dtype) for sh...]
    ppermute x16, starting transfers between devices: 25.6 us -> 28.6 us  [per_device(): came = lax.ppermute(held, 'ka', pairs)]
  transfers between devices with their start and end apart: 56 -> 56, of which waited for: 39 -> 37; matrix products, arithmetic and copies ran while one was open for 1% -> 1% of each run, Pallas kernels for 11% -> 12%
where the time goes in v1:
time: 231 us
  waiting for transfers between devices  116 us (50%)
  starting transfers between devices  65.5 us (28%)
  Pallas kernels  43.9 us (19%)
  other arithmetic  3.54 us (2%)
    ppermute x16, waiting for transfers between devices, per_device(): came = lax.ppermute(held, 'ka', pairs)  54 us
    pallas_call x29, Pallas kernels, call(): pl.pallas_call(body, out_shape=[jax.ShapeDtypeStruct(shape, dtype) for sh...  39.1 us
    ppermute x16, starting transfers between devices, per_device(): came = lax.ppermute(held, 'ka', pairs)  28.6 us
    ppermute x8, waiting for transfers between devices, per_device(): y_own = y_own + lax.ppermute(y_own, both, pairs)  22 us
    ppermute x8, waiting for transfers between devices, per_device(): y_part = lax.ppermute(y_part, both, first_round)  16.1 us
    ppermute x8, starting transfers between devices, per_device(): y_own = y_own + lax.ppermute(y_own, both, pairs)  15.8 us
    ppermute x8, waiting for transfers between devices, per_device(): lax.ppermute(send[at], both, first_round)  15.4 us
    ppermute x8, starting transfers between devices, per_device(): lax.ppermute(send[at], both, first_round)  8.63 us
  transfers between devices with their start and end apart: 56, of which 37 were waited for; matrix products, arithmetic and copies ran while one was open for 1% of the time, Pallas kernels for 12%

profile of v1, /device:TPU:0, one launch (start us, length us, event | category | flops | bytes accessed | tf_op | source)
XLA Modules:
  0.0 231.2 jit_solution(14017923139242097908)
XLA Ops:
  0.7 4.8 %shard_map.67 = (bf16[2,1024,2048]{2,1,0:T(8,128)(2,1)S(1)}, bf16[2,2048,1024]{2,1,0:T(8,128)(2,1)S(1)}) custom-call(s32[4]{0:T(128)S(1)} %pad_add_fusion.own_ref, f32[1024,2048]{1,0:T(8,128)} %m_ref.1), custom_call_target="tpu_custom_call" | custom-call | flops 2147483648 | tf_op jit(solution)/shard_map/pallas_call | solution.py:317
  5.8 1.9 shard_map.68
  8.2 1.8 shard_map.69
  10.1 2.6 %collective-permute-start.3 = (f32[648,128]{1,0:T(8,128)S(1)}, f32[648,128]{1,0:T(8,128)S(1)}, u32[]{:S(2)}, u32[]{:S(2)}) collective-permute-start(f32[648,128]{1,0:T(8,128)S(1)} %slice_add_fusion.3), channel_id=1, source_target_pairs={{0,8},{4,20},{8,0},{12,28},{16,24},{20,4},{24,16},{28,12},{1,9},{5... | collective-permute-start | bytes 995336 | tf_op jit(solution)/shard_map/ppermute | solution.py:397
  12.7 5.1 %collective-permute-done.3 = f32[648,128]{1,0:T(8,128)S(1)} collective-permute-done((f32[648,128]{1,0:T(8,128)S(1)}, f32[648,128]{1,0:T(8,128)S(1)}, u32[]{:S(2)}, u32[]{:S(2)}) %collective-permute-start.3) | collective-permute-done | bytes 331808 | tf_op jit(solution)/shard_map/ppermute | solution.py:397
  17.9 2.1 collective-permute-start.4
  21.6 4.5 %collective-permute-done.1 = f32[384,128]{1,0:T(8,128)S(1)} collective-permute-done((f32[384,128]{1,0:T(8,128)S(1)}, f32[384,128]{1,0:T(8,128)S(1)}, u32[]{:S(2)}, u32[]{:S(2)}) %collective-permute-start.1) | collective-permute-done | bytes 196640 | tf_op jit(solution)/shard_map/ppermute | solution.py:397
  26.1 1.8 collective-permute-start.2
  28.0 3.8 %collective-permute-done.2 = f32[384,128]{1,0:T(8,128)S(1)} collective-permute-done((f32[384,128]{1,0:T(8,128)S(1)}, f32[384,128]{1,0:T(8,128)S(1)}, u32[]{:S(2)}, u32[]{:S(2)}) %collective-permute-start.2) | collective-permute-done | bytes 196640 | tf_op jit(solution)/shard_map/ppermute | solution.py:397
  36.2 1.9 collective-permute-start.9
  39.7 2.9 %collective-permute-done.9 = f32[264,128]{1,0:T(8,128)S(1)} collective-permute-done((f32[264,128]{1,0:T(8,128)S(1)}, f32[264,128]{1,0:T(8,128)S(1)}, u32[]{:S(2)}, u32[]{:S(2)}) %collective-permute-start.9) | collective-permute-done | bytes 135200 | tf_op jit(solution)/shard_map/ppermute | solution.py:421
  42.6 3.0 %collective-permute-start.10 = (f32[264,128]{1,0:T(8,128)S(1)}, f32[264,128]{1,0:T(8,128)S(1)}, u32[]{:S(2)}, u32[]{:S(2)}) collective-permute-start(f32[264,128]{1,0:T(8,128)S(1)} %slice_add_fusion.11), channel_id=1, source_target_pairs={{0,2},{1,3},{2,0},{3,1},{4,5},{5,4},{6,7},{7,6},{8,10},{9,11},{10,... | collective-permute-start | bytes 405512 | tf_op jit(solution)/shard_map/ppermute | solution.py:427
  45.6 2.3 collective-permute-start.8
  47.9 5.0 %collective-permute-done.8 = f32[256,128]{1,0:T(8,128)S(1)} collective-permute-done((f32[256,128]{1,0:T(8,128)S(1)}, f32[256,128]{1,0:T(8,128)S(1)}, u32[]{:S(2)}, u32[]{:S(2)}) %collective-permute-start.8) | collective-permute-done | bytes 131104 | tf_op jit(solution)/shard_map/ppermute | solution.py:427
  55.2 1.9 shard_map.74
  57.0 2.5 %collective-permute-done.11 = f32[256,128]{1,0:T(8,128)S(1)} collective-permute-done((f32[256,128]{1,0:T(8,128)S(1)}, f32[256,128]{1,0:T(8,128)S(1)}, u32[]{:S(2)}, u32[]{:S(2)}) %collective-permute-start.11) | collective-permute-done | bytes 131104 | tf_op jit(solution)/shard_map/ppermute | solution.py:429
  59.6 1.9 collective-permute-done.12
  64.8 1.9 collective-permute-start.16
  66.7 5.3 %collective-permute-done.16 = f32[648,128]{1,0:T(8,128)S(1)} collective-permute-done((f32[648,128]{1,0:T(8,128)S(1)}, f32[648,128]{1,0:T(8,128)S(1)}, u32[]{:S(2)}, u32[]{:S(2)}) %collective-permute-start.16) | collective-permute-done | bytes 331808 | tf_op jit(solution)/shard_map/ppermute | solution.py:397
  72.1 1.9 collective-permute-start.17
  75.6 4.2 %collective-permute-done.14 = f32[384,128]{1,0:T(8,128)S(1)} collective-permute-done((f32[384,128]{1,0:T(8,128)S(1)}, f32[384,128]{1,0:T(8,128)S(1)}, u32[]{:S(2)}, u32[]{:S(2)}) %collective-permute-start.14) | collective-permute-done | bytes 196640 | tf_op jit(solution)/shard_map/ppermute | solution.py:397
  79.8 1.8 collective-permute-start.15
  81.7 3.8 %collective-permute-done.15 = f32[384,128]{1,0:T(8,128)S(1)} collective-permute-done((f32[384,128]{1,0:T(8,128)S(1)}, f32[384,128]{1,0:T(8,128)S(1)}, u32[]{:S(2)}, u32[]{:S(2)}) %collective-permute-start.15) | collective-permute-done | bytes 196640 | tf_op jit(solution)/shard_map/ppermute | solution.py:397
  93.2 3.4 %collective-permute-done.22 = f32[264,128]{1,0:T(8,128)S(1)} collective-permute-done((f32[264,128]{1,0:T(8,128)S(1)}, f32[264,128]{1,0:T(8,128)S(1)}, u32[]{:S(2)}, u32[]{:S(2)}) %collective-permute-start.22) | collective-permute-done | bytes 135200 | tf_op jit(solution)/shard_map/ppermute | solution.py:421
  96.7 1.9 collective-permute-start.23
  99.4 1.7 collective-permute-start.21
  101.2 5.3 %collective-permute-done.21 = f32[256,128]{1,0:T(8,128)S(1)} collective-permute-done((f32[256,128]{1,0:T(8,128)S(1)}, f32[256,128]{1,0:T(8,128)S(1)}, u32[]{:S(2)}, u32[]{:S(2)}) %collective-permute-start.21) | collective-permute-done | bytes 131104 | tf_op jit(solution)/shard_map/ppermute | solution.py:427
  108.8 1.9 shard_map.81
  110.6 3.0 %collective-permute-done.24 = f32[256,128]{1,0:T(8,128)S(1)} collective-permute-done((f32[256,128]{1,0:T(8,128)S(1)}, f32[256,128]{1,0:T(8,128)S(1)}, u32[]{:S(2)}, u32[]{:S(2)}) %collective-permute-start.24) | collective-permute-done | bytes 131104 | tf_op jit(solution)/shard_map/ppermute | solution.py:429
  120.2 5.6 %collective-permute-done.29 = f32[648,128]{1,0:T(8,128)S(1)} collective-permute-done((f32[648,128]{1,0:T(8,128)S(1)}, f32[648,128]{1,0:T(8,128)S(1)}, u32[]{:S(2)}, u32[]{:S(2)}) %collective-permute-start.29) | collective-permute-done | bytes 331808 | tf_op jit(solution)/shard_map/ppermute | solution.py:397
  129.2 4.3 %collective-permute-done.27 = f32[384,128]{1,0:T(8,128)S(1)} collective-permute-done((f32[384,128]{1,0:T(8,128)S(1)}, f32[384,128]{1,0:T(8,128)S(1)}, u32[]{:S(2)}, u32[]{:S(2)}) %collective-permute-start.27) | collective-permute-done | bytes 196640 | tf_op jit(solution)/shard_map/ppermute | solution.py:397
  135.3 3.9 %collective-permute-done.28 = f32[384,128]{1,0:T(8,128)S(1)} collective-permute-done((f32[384,128]{1,0:T(8,128)S(1)}, f32[384,128]{1,0:T(8,128)S(1)}, u32[]{:S(2)}, u32[]{:S(2)}) %collective-permute-start.28) | collective-permute-done | bytes 196640 | tf_op jit(solution)/shard_map/ppermute | solution.py:397
  143.6 1.9 collective-permute-start.33
  146.7 3.2 %collective-permute-done.35 = f32[264,128]{1,0:T(8,128)S(1)} collective-permute-done((f32[264,128]{1,0:T(8,128)S(1)}, f32[264,128]{1,0:T(8,128)S(1)}, u32[]{:S(2)}, u32[]{:S(2)}) %collective-permute-start.35) | collective-permute-done | bytes 135200 | tf_op jit(solution)/shard_map/ppermute | solution.py:421
  149.9 1.9 collective-permute-start.36
  154.4 5.8 %collective-permute-done.34 = f32[256,128]{1,0:T(8,128)S(1)} collective-permute-done((f32[256,128]{1,0:T(8,128)S(1)}, f32[256,128]{1,0:T(8,128)S(1)}, u32[]{:S(2)}, u32[]{:S(2)}) %collective-permute-start.34) | collective-permute-done | bytes 131104 | tf_op jit(solution)/shard_map/ppermute | solution.py:427
  162.5 1.9 shard_map.88
  164.3 2.8 %collective-permute-done.37 = f32[256,128]{1,0:T(8,128)S(1)} collective-permute-done((f32[256,128]{1,0:T(8,128)S(1)}, f32[256,128]{1,0:T(8,128)S(1)}, u32[]{:S(2)}, u32[]{:S(2)}) %collective-permute-start.37) | collective-permute-done | bytes 131104 | tf_op jit(solution)/shard_map/ppermute | solution.py:429
  173.6 5.5 %collective-permute-done.42 = f32[648,128]{1,0:T(8,128)S(1)} collective-permute-done((f32[648,128]{1,0:T(8,128)S(1)}, f32[648,128]{1,0:T(8,128)S(1)}, u32[]{:S(2)}, u32[]{:S(2)}) %collective-permute-start.42) | collective-permute-done | bytes 331808 | tf_op jit(solution)/shard_map/ppermute | solution.py:397
  180.8 1.8 collective-permute-start.40
  182.6 4.1 %collective-permute-done.40 = f32[384,128]{1,0:T(8,128)S(1)} collective-permute-done((f32[384,128]{1,0:T(8,128)S(1)}, f32[384,128]{1,0:T(8,128)S(1)}, u32[]{:S(2)}, u32[]{:S(2)}) %collective-permute-start.40) | collective-permute-done | bytes 196640 | tf_op jit(solution)/shard_map/ppermute | solution.py:397
  188.6 3.9 %collective-permute-done.41 = f32[384,128]{1,0:T(8,128)S(1)} collective-permute-done((f32[384,128]{1,0:T(8,128)S(1)}, f32[384,128]{1,0:T(8,128)S(1)}, u32[]{:S(2)}, u32[]{:S(2)}) %collective-permute-start.41) | collective-permute-done | bytes 196640 | tf_op jit(solution)/shard_map/ppermute | solution.py:397
  197.3 1.7 collective-permute-start.46
  200.3 3.0 %collective-permute-done.48 = f32[264,128]{1,0:T(8,128)S(1)} collective-permute-done((f32[264,128]{1,0:T(8,128)S(1)}, f32[264,128]{1,0:T(8,128)S(1)}, u32[]{:S(2)}, u32[]{:S(2)}) %collective-permute-start.48) | collective-permute-done | bytes 135200 | tf_op jit(solution)/shard_map/ppermute | solution.py:421
  203.3 1.9 collective-permute-start.49
  207.8 5.8 %collective-permute-done.47 = f32[256,128]{1,0:T(8,128)S(1)} collective-permute-done((f32[256,128]{1,0:T(8,128)S(1)}, f32[256,128]{1,0:T(8,128)S(1)}, u32[]{:S(2)}, u32[]{:S(2)}) %collective-permute-start.47) | collective-permute-done | bytes 131104 | tf_op jit(solution)/shard_map/ppermute | solution.py:427
  214.9 3.1 %collective-permute-done.50 = f32[8,128]{1,0:T(8,128)S(1)} collective-permute-done((f32[8,128]{1,0:T(8,128)S(1)}, f32[8,128]{1,0:T(8,128)S(1)}, u32[]{:S(2)}, u32[]{:S(2)}) %collective-permute-start.50) | collective-permute-done | bytes 4128 | tf_op jit(solution)/shard_map/ppermute | solution.py:434
  227.0 2.8 %collective-permute-done.55 = f32[256,128]{1,0:T(8,128)S(1)} collective-permute-done((f32[256,128]{1,0:T(8,128)S(1)}, f32[256,128]{1,0:T(8,128)S(1)}, u32[]{:S(2)}, u32[]{:S(2)}) %collective-permute-start.55) | collective-permute-done | bytes 131104 | tf_op jit(solution)/shard_map/ppermute | solution.py:429
  (183 shorter events, 79.3 us)
Async XLA Ops:
  10.1 7.7 %collective-permute-start.3 = (f32[648,128]{1,0:T(8,128)S(1)}, f32[648,128]{1,0:T(8,128)S(1)}, u32[]{:S(2)}, u32[]{:S(2)}) collective-permute-start(f32[648,128]{1,0:T(8,128)S(1)} %slice_add_fusion.3), channel_id=1, source_target_pairs={{0,8},{4,20},{8,0},{12,28},{16,24},{20,4},{24,16},{28,12},{1,9},{5... | collective-permute-start | bytes 995336 | tf_op jit(solution)/shard_map/ppermute | solution.py:397
  17.9 10.0 %collective-permute-start.4 = (f32[648,128]{1,0:T(8,128)S(1)}, f32[648,128]{1,0:T(8,128)S(1)}, u32[]{:S(2)}, u32[]{:S(2)}) collective-permute-start(f32[648,128]{1,0:T(8,128)S(1)} %add.142), channel_id=1, source_target_pairs={{0,16},{4,12},{8,24},{12,4},{16,0},{20,28},{24,8},{28,20},{1,17},{... | collective-permute-start | bytes 995336 | tf_op jit(solution)/shard_map/ppermute | solution.py:397
  20.0 6.0 %collective-permute-start.1 = (f32[384,128]{1,0:T(8,128)S(1)}, f32[384,128]{1,0:T(8,128)S(1)}, u32[]{:S(2)}, u32[]{:S(2)}) collective-permute-start(f32[384,128]{1,0:T(8,128)S(1)} %slice_add_fusion.7), channel_id=1, source_target_pairs={{0,8},{4,20},{8,0},{12,28},{16,24},{20,4},{24,16},{28,12},{1,9},{5... | collective-permute-start | bytes 589832 | tf_op jit(solution)/shard_map/ppermute | solution.py:397
  26.1 5.7 %collective-permute-start.2 = (f32[384,128]{1,0:T(8,128)S(1)}, f32[384,128]{1,0:T(8,128)S(1)}, u32[]{:S(2)}, u32[]{:S(2)}) collective-permute-start(f32[384,128]{1,0:T(8,128)S(1)} %add.139), channel_id=1, source_target_pairs={{0,16},{4,12},{8,24},{12,4},{16,0},{20,28},{24,8},{28,20},{1,17},{... | collective-permute-start | bytes 589832 | tf_op jit(solution)/shard_map/ppermute | solution.py:397
  28.0 6.9 %collective-permute-start.6 = (f32[640,128]{1,0:T(8,128)S(1)}, f32[640,128]{1,0:T(8,128)S(1)}, u32[]{:S(2)}, u32[]{:S(2)}) collective-permute-start(f32[640,128]{1,0:T(8,128)S(1)} %slice.180), channel_id=1, source_target_pairs={{0,4},{4,0},{8,12},{12,8},{16,20},{20,16},{24,28},{28,24},{1,5},{5... | collective-permute-start | bytes 983048 | tf_op jit(solution)/shard_map/ppermute | solution.py:399
  31.8 3.0 %collective-permute-start.5 = (f32[384,128]{1,0:T(8,128)S(1)}, f32[384,128]{1,0:T(8,128)S(1)}, u32[]{:S(2)}, u32[]{:S(2)}) collective-permute-start(f32[384,128]{1,0:T(8,128)S(1)} %add.140.held_ref), channel_id=1, source_target_pairs={{0,4},{4,0},{8,12},{12,8},{16,20},{20,16},{24,28},{28,24},{1,5},{5... | collective-permute-start | bytes 589832 | tf_op jit(solution)/shard_map/ppermute | solution.py:399
  36.2 6.3 %collective-permute-start.9 = (f32[264,128]{1,0:T(8,128)S(1)}, f32[264,128]{1,0:T(8,128)S(1)}, u32[]{:S(2)}, u32[]{:S(2)}) collective-permute-start(f32[264,128]{1,0:T(8,128)S(1)} %slice.140), channel_id=1, source_target_pairs={{0,1},{1,0},{2,3},{3,2},{4,6},{5,7},{6,4},{7,5},{8,9},{9,8},{10,11... | collective-permute-start | bytes 405512 | tf_op jit(solution)/shard_map/ppermute | solution.py:421
  38.1 7.5 %collective-permute-start.7 = (f32[256,128]{1,0:T(8,128)S(1)}, f32[256,128]{1,0:T(8,128)S(1)}, u32[]{:S(2)}, u32[]{:S(2)}) collective-permute-start(f32[256,128]{1,0:T(8,128)S(1)} %slice.138), channel_id=1, source_target_pairs={{0,1},{1,0},{2,3},{3,2},{4,6},{5,7},{6,4},{7,5},{8,9},{9,8},{10,11... | collective-permute-start | bytes 393224 | tf_op jit(solution)/shard_map/ppermute | solution.py:421
  42.6 11.7 %collective-permute-start.10 = (f32[264,128]{1,0:T(8,128)S(1)}, f32[264,128]{1,0:T(8,128)S(1)}, u32[]{:S(2)}, u32[]{:S(2)}) collective-permute-start(f32[264,128]{1,0:T(8,128)S(1)} %slice_add_fusion.11), channel_id=1, source_target_pairs={{0,2},{1,3},{2,0},{3,1},{4,5},{5,4},{6,7},{7,6},{8,10},{9,11},{10,... | collective-permute-start | bytes 405512 | tf_op jit(solution)/shard_map/ppermute | solution.py:427
  45.6 7.3 %collective-permute-start.8 = (f32[256,128]{1,0:T(8,128)S(1)}, f32[256,128]{1,0:T(8,128)S(1)}, u32[]{:S(2)}, u32[]{:S(2)}) collective-permute-start(f32[256,128]{1,0:T(8,128)S(1)} %slice_add_fusion.15), channel_id=1, source_target_pairs={{0,2},{1,3},{2,0},{3,1},{4,5},{5,4},{6,7},{7,6},{8,10},{9,11},{10,... | collective-permute-start | bytes 393224 | tf_op jit(solution)/shard_map/ppermute | solution.py:427
  52.9 6.6 %collective-permute-start.11 = (f32[256,128]{1,0:T(8,128)S(1)}, f32[256,128]{1,0:T(8,128)S(1)}, u32[]{:S(2)}, u32[]{:S(2)}) collective-permute-start(f32[256,128]{1,0:T(8,128)S(1)} %add.145), channel_id=1, source_target_pairs={{0,1},{1,0},{2,3},{3,2},{4,6},{5,7},{6,4},{7,5},{8,9},{9,8},{10,11... | collective-permute-start | bytes 393224 | tf_op jit(solution)/shard_map/ppermute | solution.py:429
  54.3 7.1 %collective-permute-start.12 = (f32[256,128]{1,0:T(8,128)S(1)}, f32[256,128]{1,0:T(8,128)S(1)}, u32[]{:S(2)}, u32[]{:S(2)}) collective-permute-start(f32[256,128]{1,0:T(8,128)S(1)} %slice.183), channel_id=1, source_target_pairs={{0,1},{1,0},{2,3},{3,2},{4,6},{5,7},{6,4},{7,5},{8,9},{9,8},{10,11... | collective-permute-start | bytes 393224 | tf_op jit(solution)/shard_map/ppermute | solution.py:429
  64.8 7.2 %collective-permute-start.16 = (f32[648,128]{1,0:T(8,128)S(1)}, f32[648,128]{1,0:T(8,128)S(1)}, u32[]{:S(2)}, u32[]{:S(2)}) collective-permute-start(f32[648,128]{1,0:T(8,128)S(1)} %slice_add_fusion.2), channel_id=1, source_target_pairs={{0,8},{4,20},{8,0},{12,28},{16,24},{20,4},{24,16},{28,12},{1,9},{5... | collective-permute-start | bytes 995336 | tf_op jit(solution)/shard_map/ppermute | solution.py:397
  72.1 9.5 %collective-permute-start.17 = (f32[648,128]{1,0:T(8,128)S(1)}, f32[648,128]{1,0:T(8,128)S(1)}, u32[]{:S(2)}, u32[]{:S(2)}) collective-permute-start(f32[648,128]{1,0:T(8,128)S(1)} %add.152), channel_id=1, source_target_pairs={{0,16},{4,12},{8,24},{12,4},{16,0},{20,28},{24,8},{28,20},{1,17},{... | collective-permute-start | bytes 995336 | tf_op jit(solution)/shard_map/ppermute | solution.py:397
  74.0 5.8 %collective-permute-start.14 = (f32[384,128]{1,0:T(8,128)S(1)}, f32[384,128]{1,0:T(8,128)S(1)}, u32[]{:S(2)}, u32[]{:S(2)}) collective-permute-start(f32[384,128]{1,0:T(8,128)S(1)} %slice_add_fusion.6), channel_id=1, source_target_pairs={{0,8},{4,20},{8,0},{12,28},{16,24},{20,4},{24,16},{28,12},{1,9},{5... | collective-permute-start | bytes 589832 | tf_op jit(solution)/shard_map/ppermute | solution.py:397
  79.8 5.7 %collective-permute-start.15 = (f32[384,128]{1,0:T(8,128)S(1)}, f32[384,128]{1,0:T(8,128)S(1)}, u32[]{:S(2)}, u32[]{:S(2)}) collective-permute-start(f32[384,128]{1,0:T(8,128)S(1)} %add.149), channel_id=1, source_target_pairs={{0,16},{4,12},{8,24},{12,4},{16,0},{20,28},{24,8},{28,20},{1,17},{... | collective-permute-start | bytes 589832 | tf_op jit(solution)/shard_map/ppermute | solution.py:397
  81.7 6.8 %collective-permute-start.19 = (f32[640,128]{1,0:T(8,128)S(1)}, f32[640,128]{1,0:T(8,128)S(1)}, u32[]{:S(2)}, u32[]{:S(2)}) collective-permute-start(f32[640,128]{1,0:T(8,128)S(1)} %slice.188), channel_id=1, source_target_pairs={{0,4},{4,0},{8,12},{12,8},{16,20},{20,16},{24,28},{28,24},{1,5},{5... | collective-permute-start | bytes 983048 | tf_op jit(solution)/shard_map/ppermute | solution.py:399
  89.8 6.8 %collective-permute-start.22 = (f32[264,128]{1,0:T(8,128)S(1)}, f32[264,128]{1,0:T(8,128)S(1)}, u32[]{:S(2)}, u32[]{:S(2)}) collective-permute-start(f32[264,128]{1,0:T(8,128)S(1)} %slice.150), channel_id=1, source_target_pairs={{0,1},{1,0},{2,3},{3,2},{4,6},{5,7},{6,4},{7,5},{8,9},{9,8},{10,11... | collective-permute-start | bytes 405512 | tf_op jit(solution)/shard_map/ppermute | solution.py:421
  90.8 8.6 %collective-permute-start.20 = (f32[256,128]{1,0:T(8,128)S(1)}, f32[256,128]{1,0:T(8,128)S(1)}, u32[]{:S(2)}, u32[]{:S(2)}) collective-permute-start(f32[256,128]{1,0:T(8,128)S(1)} %slice.148), channel_id=1, source_target_pairs={{0,1},{1,0},{2,3},{3,2},{4,6},{5,7},{6,4},{7,5},{8,9},{9,8},{10,11... | collective-permute-start | bytes 393224 | tf_op jit(solution)/shard_map/ppermute | solution.py:421
  96.7 10.9 %collective-permute-start.23 = (f32[264,128]{1,0:T(8,128)S(1)}, f32[264,128]{1,0:T(8,128)S(1)}, u32[]{:S(2)}, u32[]{:S(2)}) collective-permute-start(f32[264,128]{1,0:T(8,128)S(1)} %slice_add_fusion.10), channel_id=1, source_target_pairs={{0,2},{1,3},{2,0},{3,1},{4,5},{5,4},{6,7},{7,6},{8,10},{9,11},{10,... | collective-permute-start | bytes 405512 | tf_op jit(solution)/shard_map/ppermute | solution.py:427
  99.4 7.1 %collective-permute-start.21 = (f32[256,128]{1,0:T(8,128)S(1)}, f32[256,128]{1,0:T(8,128)S(1)}, u32[]{:S(2)}, u32[]{:S(2)}) collective-permute-start(f32[256,128]{1,0:T(8,128)S(1)} %slice_add_fusion.14), channel_id=1, source_target_pairs={{0,2},{1,3},{2,0},{3,1},{4,5},{5,4},{6,7},{7,6},{8,10},{9,11},{10,... | collective-permute-start | bytes 393224 | tf_op jit(solution)/shard_map/ppermute | solution.py:427
  106.5 7.1 %collective-permute-start.24 = (f32[256,128]{1,0:T(8,128)S(1)}, f32[256,128]{1,0:T(8,128)S(1)}, u32[]{:S(2)}, u32[]{:S(2)}) collective-permute-start(f32[256,128]{1,0:T(8,128)S(1)} %add.155), channel_id=1, source_target_pairs={{0,1},{1,0},{2,3},{3,2},{4,6},{5,7},{6,4},{7,5},{8,9},{9,8},{10,11... | collective-permute-start | bytes 393224 | tf_op jit(solution)/shard_map/ppermute | solution.py:429
  107.6 7.7 %collective-permute-start.25 = (f32[256,128]{1,0:T(8,128)S(1)}, f32[256,128]{1,0:T(8,128)S(1)}, u32[]{:S(2)}, u32[]{:S(2)}) collective-permute-start(f32[256,128]{1,0:T(8,128)S(1)} %slice.191), channel_id=1, source_target_pairs={{0,1},{1,0},{2,3},{3,2},{4,6},{5,7},{6,4},{7,5},{8,9},{9,8},{10,11... | collective-permute-start | bytes 393224 | tf_op jit(solution)/shard_map/ppermute | solution.py:429
  118.6 7.2 %collective-permute-start.29 = (f32[648,128]{1,0:T(8,128)S(1)}, f32[648,128]{1,0:T(8,128)S(1)}, u32[]{:S(2)}, u32[]{:S(2)}) collective-permute-start(f32[648,128]{1,0:T(8,128)S(1)} %slice_add_fusion.1), channel_id=1, source_target_pairs={{0,8},{4,20},{8,0},{12,28},{16,24},{20,4},{24,16},{28,12},{1,9},{5... | collective-permute-start | bytes 995336 | tf_op jit(solution)/shard_map/ppermute | solution.py:397
  125.9 9.3 %collective-permute-start.30 = (f32[648,128]{1,0:T(8,128)S(1)}, f32[648,128]{1,0:T(8,128)S(1)}, u32[]{:S(2)}, u32[]{:S(2)}) collective-permute-start(f32[648,128]{1,0:T(8,128)S(1)} %add.162), channel_id=1, source_target_pairs={{0,16},{4,12},{8,24},{12,4},{16,0},{20,28},{24,8},{28,20},{1,17},{... | collective-permute-start | bytes 995336 | tf_op jit(solution)/shard_map/ppermute | solution.py:397
  127.5 5.9 %collective-permute-start.27 = (f32[384,128]{1,0:T(8,128)S(1)}, f32[384,128]{1,0:T(8,128)S(1)}, u32[]{:S(2)}, u32[]{:S(2)}) collective-permute-start(f32[384,128]{1,0:T(8,128)S(1)} %slice_add_fusion.5), channel_id=1, source_target_pairs={{0,8},{4,20},{8,0},{12,28},{16,24},{20,4},{24,16},{28,12},{1,9},{5... | collective-permute-start | bytes 589832 | tf_op jit(solution)/shard_map/ppermute | solution.py:397
  133.5 5.7 %collective-permute-start.28 = (f32[384,128]{1,0:T(8,128)S(1)}, f32[384,128]{1,0:T(8,128)S(1)}, u32[]{:S(2)}, u32[]{:S(2)}) collective-permute-start(f32[384,128]{1,0:T(8,128)S(1)} %add.159), channel_id=1, source_target_pairs={{0,16},{4,12},{8,24},{12,4},{16,0},{20,28},{24,8},{28,20},{1,17},{... | collective-permute-start | bytes 589832 | tf_op jit(solution)/shard_map/ppermute | solution.py:397
  135.2 6.8 %collective-permute-start.32 = (f32[640,128]{1,0:T(8,128)S(1)}, f32[640,128]{1,0:T(8,128)S(1)}, u32[]{:S(2)}, u32[]{:S(2)}) collective-permute-start(f32[640,128]{1,0:T(8,128)S(1)} %slice.196), channel_id=1, source_target_pairs={{0,4},{4,0},{8,12},{12,8},{16,20},{20,16},{24,28},{28,24},{1,5},{5... | collective-permute-start | bytes 983048 | tf_op jit(solution)/shard_map/ppermute | solution.py:399
  143.3 6.6 %collective-permute-start.35 = (f32[264,128]{1,0:T(8,128)S(1)}, f32[264,128]{1,0:T(8,128)S(1)}, u32[]{:S(2)}, u32[]{:S(2)}) collective-permute-start(f32[264,128]{1,0:T(8,128)S(1)} %slice.160), channel_id=1, source_target_pairs={{0,1},{1,0},{2,3},{3,2},{4,6},{5,7},{6,4},{7,5},{8,9},{9,8},{10,11... | collective-permute-start | bytes 405512 | tf_op jit(solution)/shard_map/ppermute | solution.py:421
  143.6 9.3 %collective-permute-start.33 = (f32[256,128]{1,0:T(8,128)S(1)}, f32[256,128]{1,0:T(8,128)S(1)}, u32[]{:S(2)}, u32[]{:S(2)}) collective-permute-start(f32[256,128]{1,0:T(8,128)S(1)} %slice.158), channel_id=1, source_target_pairs={{0,1},{1,0},{2,3},{3,2},{4,6},{5,7},{6,4},{7,5},{8,9},{9,8},{10,11... | collective-permute-start | bytes 393224 | tf_op jit(solution)/shard_map/ppermute | solution.py:421
  149.9 10.9 %collective-permute-start.36 = (f32[264,128]{1,0:T(8,128)S(1)}, f32[264,128]{1,0:T(8,128)S(1)}, u32[]{:S(2)}, u32[]{:S(2)}) collective-permute-start(f32[264,128]{1,0:T(8,128)S(1)} %slice_add_fusion.9), channel_id=1, source_target_pairs={{0,2},{1,3},{2,0},{3,1},{4,5},{5,4},{6,7},{7,6},{8,10},{9,11},{10,... | collective-permute-start | bytes 405512 | tf_op jit(solution)/shard_map/ppermute | solution.py:427
  152.9 7.3 %collective-permute-start.34 = (f32[256,128]{1,0:T(8,128)S(1)}, f32[256,128]{1,0:T(8,128)S(1)}, u32[]{:S(2)}, u32[]{:S(2)}) collective-permute-start(f32[256,128]{1,0:T(8,128)S(1)} %slice_add_fusion.13), channel_id=1, source_target_pairs={{0,2},{1,3},{2,0},{3,1},{4,5},{5,4},{6,7},{7,6},{8,10},{9,11},{10,... | collective-permute-start | bytes 393224 | tf_op jit(solution)/shard_map/ppermute | solution.py:427
  160.2 6.9 %collective-permute-start.37 = (f32[256,128]{1,0:T(8,128)S(1)}, f32[256,128]{1,0:T(8,128)S(1)}, u32[]{:S(2)}, u32[]{:S(2)}) collective-permute-start(f32[256,128]{1,0:T(8,128)S(1)} %add.165), channel_id=1, source_target_pairs={{0,1},{1,0},{2,3},{3,2},{4,6},{5,7},{6,4},{7,5},{8,9},{9,8},{10,11... | collective-permute-start | bytes 393224 | tf_op jit(solution)/shard_map/ppermute | solution.py:429
  160.9 7.7 %collective-permute-start.38 = (f32[256,128]{1,0:T(8,128)S(1)}, f32[256,128]{1,0:T(8,128)S(1)}, u32[]{:S(2)}, u32[]{:S(2)}) collective-permute-start(f32[256,128]{1,0:T(8,128)S(1)} %slice.199), channel_id=1, source_target_pairs={{0,1},{1,0},{2,3},{3,2},{4,6},{5,7},{6,4},{7,5},{8,9},{9,8},{10,11... | collective-permute-start | bytes 393224 | tf_op jit(solution)/shard_map/ppermute | solution.py:429
  171.9 7.2 %collective-permute-start.42 = (f32[648,128]{1,0:T(8,128)S(1)}, f32[648,128]{1,0:T(8,128)S(1)}, u32[]{:S(2)}, u32[]{:S(2)}) collective-permute-start(f32[648,128]{1,0:T(8,128)S(1)} %slice_add_fusion), channel_id=1, source_target_pairs={{0,8},{4,20},{8,0},{12,28},{16,24},{20,4},{24,16},{28,12},{1,9},{5... | collective-permute-start | bytes 995336 | tf_op jit(solution)/shard_map/ppermute | solution.py:397
  179.2 9.3 %collective-permute-start.43 = (f32[648,128]{1,0:T(8,128)S(1)}, f32[648,128]{1,0:T(8,128)S(1)}, u32[]{:S(2)}, u32[]{:S(2)}) collective-permute-start(f32[648,128]{1,0:T(8,128)S(1)} %add.172), channel_id=1, source_target_pairs={{0,16},{4,12},{8,24},{12,4},{16,0},{20,28},{24,8},{28,20},{1,17},{... | collective-permute-start | bytes 995336 | tf_op jit(solution)/shard_map/ppermute | solution.py:397
  180.8 5.9 %collective-permute-start.40 = (f32[384,128]{1,0:T(8,128)S(1)}, f32[384,128]{1,0:T(8,128)S(1)}, u32[]{:S(2)}, u32[]{:S(2)}) collective-permute-start(f32[384,128]{1,0:T(8,128)S(1)} %slice_add_fusion.4), channel_id=1, source_target_pairs={{0,8},{4,20},{8,0},{12,28},{16,24},{20,4},{24,16},{28,12},{1,9},{5... | collective-permute-start | bytes 589832 | tf_op jit(solution)/shard_map/ppermute | solution.py:397
  186.8 5.7 %collective-permute-start.41 = (f32[384,128]{1,0:T(8,128)S(1)}, f32[384,128]{1,0:T(8,128)S(1)}, u32[]{:S(2)}, u32[]{:S(2)}) collective-permute-start(f32[384,128]{1,0:T(8,128)S(1)} %add.169), channel_id=1, source_target_pairs={{0,16},{4,12},{8,24},{12,4},{16,0},{20,28},{24,8},{28,20},{1,17},{... | collective-permute-start | bytes 589832 | tf_op jit(solution)/shard_map/ppermute | solution.py:397
  188.5 7.0 %collective-permute-start.45 = (f32[640,128]{1,0:T(8,128)S(1)}, f32[640,128]{1,0:T(8,128)S(1)}, u32[]{:S(2)}, u32[]{:S(2)}) collective-permute-start(f32[640,128]{1,0:T(8,128)S(1)} %slice.204), channel_id=1, source_target_pairs={{0,4},{4,0},{8,12},{12,8},{16,20},{20,16},{24,28},{28,24},{1,5},{5... | collective-permute-start | bytes 983048 | tf_op jit(solution)/shard_map/ppermute | solution.py:399
  196.8 6.4 %collective-permute-start.48 = (f32[264,128]{1,0:T(8,128)S(1)}, f32[264,128]{1,0:T(8,128)S(1)}, u32[]{:S(2)}, u32[]{:S(2)}) collective-permute-start(f32[264,128]{1,0:T(8,128)S(1)} %slice.170), channel_id=1, source_target_pairs={{0,1},{1,0},{2,3},{3,2},{4,6},{5,7},{6,4},{7,5},{8,9},{9,8},{10,11... | collective-permute-start | bytes 405512 | tf_op jit(solution)/shard_map/ppermute | solution.py:421
  197.3 8.9 %collective-permute-start.46 = (f32[256,128]{1,0:T(8,128)S(1)}, f32[256,128]{1,0:T(8,128)S(1)}, u32[]{:S(2)}, u32[]{:S(2)}) collective-permute-start(f32[256,128]{1,0:T(8,128)S(1)} %slice.168), channel_id=1, source_target_pairs={{0,1},{1,0},{2,3},{3,2},{4,6},{5,7},{6,4},{7,5},{8,9},{9,8},{10,11... | collective-permute-start | bytes 393224 | tf_op jit(solution)/shard_map/ppermute | solution.py:421
  203.3 10.3 %collective-permute-start.49 = (f32[264,128]{1,0:T(8,128)S(1)}, f32[264,128]{1,0:T(8,128)S(1)}, u32[]{:S(2)}, u32[]{:S(2)}) collective-permute-start(f32[264,128]{1,0:T(8,128)S(1)} %slice_add_fusion.8), channel_id=1, source_target_pairs={{0,2},{1,3},{2,0},{3,1},{4,5},{5,4},{6,7},{7,6},{8,10},{9,11},{10,... | collective-permute-start | bytes 405512 | tf_op jit(solution)/shard_map/ppermute | solution.py:427
  206.2 7.3 %collective-permute-start.47 = (f32[256,128]{1,0:T(8,128)S(1)}, f32[256,128]{1,0:T(8,128)S(1)}, u32[]{:S(2)}, u32[]{:S(2)}) collective-permute-start(f32[256,128]{1,0:T(8,128)S(1)} %slice_add_fusion.12), channel_id=1, source_target_pairs={{0,2},{1,3},{2,0},{3,1},{4,5},{5,4},{6,7},{7,6},{8,10},{9,11},{10,... | collective-permute-start | bytes 393224 | tf_op jit(solution)/shard_map/ppermute | solution.py:427
  214.3 3.7 %collective-permute-start.50 = (f32[8,128]{1,0:T(8,128)S(1)}, f32[8,128]{1,0:T(8,128)S(1)}, u32[]{:S(2)}, u32[]{:S(2)}) collective-permute-start(f32[8,128]{1,0:T(8,128)S(1)} %get-tuple-element.135), channel_id=1, source_target_pairs={{0,1},{1,0},{2,3},{3,2},{4,6},{5,7},{6,4},{7,5},{8,9},{9,8},{10,11... | collective-permute-start | bytes 12296 | tf_op jit(solution)/shard_map/ppermute | solution.py:434
  219.1 3.6 %collective-permute-start.52 = (f32[8,128]{1,0:T(8,128)S(1)}, f32[8,128]{1,0:T(8,128)S(1)}, u32[]{:S(2)}, u32[]{:S(2)}) collective-permute-start(f32[8,128]{1,0:T(8,128)S(1)} %add.179), channel_id=1, source_target_pairs={{0,8},{4,12},{8,0},{12,4},{16,24},{20,28},{24,16},{28,20},{1,9},{5... | collective-permute-start | bytes 12296 | tf_op jit(solution)/shard_map/ppermute | solution.py:437
  220.3 6.7 %collective-permute-start.54 = (f32[256,128]{1,0:T(8,128)S(1)}, f32[256,128]{1,0:T(8,128)S(1)}, u32[]{:S(2)}, u32[]{:S(2)}) collective-permute-start(f32[256,128]{1,0:T(8,128)S(1)} %add.175), channel_id=1, source_target_pairs={{0,1},{1,0},{2,3},{3,2},{4,6},{5,7},{6,4},{7,5},{8,9},{9,8},{10,11... | collective-permute-start | bytes 393224 | tf_op jit(solution)/shard_map/ppermute | solution.py:429
  222.8 3.6 %collective-permute-start.53 = (f32[8,128]{1,0:T(8,128)S(1)}, f32[8,128]{1,0:T(8,128)S(1)}, u32[]{:S(2)}, u32[]{:S(2)}) collective-permute-start(f32[8,128]{1,0:T(8,128)S(1)} %add.180), channel_id=1, source_target_pairs={{0,16},{4,20},{8,24},{12,28},{16,0},{20,4},{24,8},{28,12},{1,17},{... | collective-permute-start | bytes 12296 | tf_op jit(solution)/shard_map/ppermute | solution.py:437
  224.5 5.3 %collective-permute-start.55 = (f32[256,128]{1,0:T(8,128)S(1)}, f32[256,128]{1,0:T(8,128)S(1)}, u32[]{:S(2)}, u32[]{:S(2)}) collective-permute-start(f32[256,128]{1,0:T(8,128)S(1)} %slice.207), channel_id=1, source_target_pairs={{0,1},{1,0},{2,3},{3,2},{4,6},{5,7},{6,4},{7,5},{8,9},{9,8},{10,11... | collective-permute-start | bytes 393224 | tf_op jit(solution)/shard_map/ppermute | solution.py:429
  (11 other events, 52.3 us)
